TPU v7x, 512 devices: a whole 4x8x8 slice. The times are simulated.
512 devices in a mesh: band: 16 (over x, z_hi), fft: 32 (over y, z_lo, core).
Axes of the slice: x: 4, y: 8, z: 8 (z_hi: 4, z_lo: 2; z = z_hi * 2 + z_lo), core: 2. Of those that a mesh axis runs over, the one named last changes fastest.
Arguments:
- wave: float32 [2, 32, 128, 128, 128], P(None, 'band', 'fft'), may hold values from -6 to 6
- previous: float32 [2, 32, 128, 128, 128], P(None, 'band', 'fft'), may hold values from -6 to 6
- potential: float32 [128, 128, 128], P('band', 'fft'), may hold values from -1.5 to 1.5
- column_extent: int32 [128, 128], P('fft'), may hold values from -1 to 31, as said below
- metric: float32 [3], replicated, may hold values from 0.5 to 2
- center: float32 [1], replicated, may hold values from 0.5 to 2
- halfwidth: float32 [1], replicated, may hold values from 1 to 3
Outputs:
- filtered: float32 [2, 32, 128, 128, 128], P(None, 'band', 'fft')
Inputs may be any that keep to these rules, and one draw needn't show every extreme that they name: `column_extent`: every entry is -1 where |s(gx)| >= 32 or |s(gy)| >= 32, with s the signed index of the steps. Some column reaches the maximum.
All inputs are finite; a program needn't handle non-finite values.
Results may differ from a plain program's by a relative error of at most 0.00005.
Values sent between devices are 32-bit elements; how exact they have to be, the bound alone decides.
A program may use at most 64 MiB of HBM per device.

v0:
```python
import math

import jax
import jax.numpy as jnp
from jax import lax
from jax.sharding import PartitionSpec as P

NX = 128
NY = 128
NZ = 128


def from_everyone(value, axis):
    copies = jnp.broadcast_to(value, (lax.axis_size(axis), *value.shape))
    return lax.all_to_all(copies, axis, split_axis=0, concat_axis=0, tiled=True)


def in_order(tiles, dim):
    dims = list(tiles.shape[1:])
    dims[dim] *= tiles.shape[0]
    return jnp.moveaxis(tiles, 0, dim).reshape(dims)


def gather_directly(value, axis, dim):
    tiles = from_everyone(value, axis)
    return in_order(tiles, dim)


def signed(length):
    indices = jnp.arange(length, dtype=jnp.int32)
    return jnp.where(indices < length // 2, indices, indices - length)


def tables(length, forward):
    indices = jnp.arange(length, dtype=jnp.int32)
    phases = indices[:, None] * indices[None, :] % length
    angles = phases.astype(jnp.float32) * (2.0 * math.pi / length)
    cosine_table = jnp.cos(angles)
    sine_table = jnp.sin(angles)
    if forward:
        return (cosine_table / length, -sine_table / length)
    return (cosine_table, sine_table)


def transform(real_part, imag_part, cosine_table, sine_table, form):
    highest = lax.Precision.HIGHEST
    real_cos = jnp.einsum(form, real_part, cosine_table, precision=highest)
    imag_sin = jnp.einsum(form, imag_part, sine_table, precision=highest)
    real_sin = jnp.einsum(form, real_part, sine_table, precision=highest)
    imag_cos = jnp.einsum(form, imag_part, cosine_table, precision=highest)
    return (real_cos - imag_sin, real_sin + imag_cos)


def local(wave, previous, potential, column_extent, metric, center, halfwidth):
    gx_local = wave.shape[2]
    quarter = NY // 4
    keep_mask = (jnp.abs(signed(NZ))[None, :, None] <= column_extent[:, None, :]).astype(
        jnp.float32
    )
    coeff_real = wave[0] * keep_mask
    coeff_imag = wave[1] * keep_mask
    inverse_z = tables(NZ, False)
    real_part, imag_part = transform(
        coeff_real, coeff_imag, inverse_z[0], inverse_z[1], "bxgy,gz->bxzy"
    )
    full_potential = gather_directly(potential, "band", 0)
    inverse_x = tables(NX, False)
    forward_x = tables(NX, True)
    inverse_y = tables(NY, False)
    forward_y = tables(NY, True)
    forward_z = tables(NZ, True)
    real_part = jnp.concatenate([real_part[..., :quarter], real_part[..., NY - quarter :]], axis=-1)
    imag_part = jnp.concatenate([imag_part[..., :quarter], imag_part[..., NY - quarter :]], axis=-1)
    inverse_y = tuple(
        (jnp.concatenate([table[:quarter], table[NY - quarter :]], axis=0) for table in inverse_y)
    )
    forward_y = tuple(
        (
            jnp.concatenate([table[:, :quarter], table[:, NY - quarter :]], axis=1)
            for table in forward_y
        )
    )
    real_in = lax.all_to_all(real_part, "fft", split_axis=2, concat_axis=1, tiled=True)
    imag_in = lax.all_to_all(imag_part, "fft", split_axis=2, concat_axis=1, tiled=True)
    real_in, imag_in = transform(real_in, imag_in, inverse_y[0], inverse_y[1], "bxzg,gy->bxzy")
    real_in, imag_in = transform(real_in, imag_in, inverse_x[0], inverse_x[1], "bgzy,gx->bxzy")
    real_in = real_in * full_potential
    imag_in = imag_in * full_potential
    real_in, imag_in = transform(real_in, imag_in, forward_x[0], forward_x[1], "bxzy,xg->bgzy")
    real_part, imag_part = transform(real_in, imag_in, forward_y[0], forward_y[1], "bgzy,yk->bgzk")
    real_part, imag_part = transform(
        lax.all_to_all(real_part, "fft", split_axis=1, concat_axis=2, tiled=True),
        lax.all_to_all(imag_part, "fft", split_axis=1, concat_axis=2, tiled=True),
        forward_z[0],
        forward_z[1],
        "bxzy,zg->bxgy",
    )
    padding = jnp.zeros(real_part.shape[:-1] + (NY - 2 * quarter,), jnp.float32)
    real_part = jnp.concatenate(
        [real_part[..., :quarter], padding, real_part[..., quarter:]], axis=-1
    )
    imag_part = jnp.concatenate(
        [imag_part[..., :quarter], padding, imag_part[..., quarter:]], axis=-1
    )
    global_x = lax.axis_index("fft") * gx_local + jnp.arange(gx_local, dtype=jnp.int32)
    signed_x = jnp.where(global_x < NX // 2, global_x, global_x - NX)
    two_pi = 2.0 * math.pi
    kinetic_x = (two_pi * signed_x.astype(jnp.float32) / NX) ** 2
    kinetic_y = (two_pi * signed(NY).astype(jnp.float32) / NY) ** 2
    kinetic_z = (two_pi * signed(NZ).astype(jnp.float32) / NZ) ** 2
    kinetic = 0.5 * (
        metric[0] * kinetic_x[:, None, None]
        + metric[2] * kinetic_z[None, :, None]
        + metric[1] * kinetic_y[None, None, :]
    )
    factor = 2.0 / halfwidth[0]
    out_real = keep_mask * (
        factor * (kinetic * coeff_real + real_part - center[0] * coeff_real) - previous[0]
    )
    out_imag = keep_mask * (
        factor * (kinetic * coeff_imag + imag_part - center[0] * coeff_imag) - previous[1]
    )
    return jnp.stack([out_real, out_imag])


def solution(mesh):
    in_specs = (
        P(None, "band", "fft", None, None),
        P(None, "band", "fft", None, None),
        P("band", "fft", None),
        P("fft", None),
        P(),
        P(),
        P(),
    )
    out_specs = P(None, "band", "fft", None, None)
    return jax.shard_map(local, mesh=mesh, in_specs=in_specs, out_specs=out_specs, check_vma=False)
```

profile of v0, /device:TPU:1, one launch (start us, length us, event | category | flops | bytes accessed | tf_op | source)
XLA Modules:
  0.0 119.7 jit_solution(16274965502704667725)
XLA Ops:
  0.0 0.8 copy.127
  0.8 0.7 broadcast_in_dim.4
  1.6 13.4 %all-to-all-start.2 = ((f32[16,8,4,128]{3,1,2,0:T(8,128)}), f32[16,8,4,128]{3,1,2,0:T(8,128)S(1)}, u32[]{:S(2)}, u32[]{:S(2)}) async-start(f32[16,8,4,128]{3,1,2,0:T(8,128)} %broadcast_in_dim.4), calls=%async_computation.2 | async-start | bytes 524288 | tf_op jit(solution)/shard_map/all_to_all | solution.py:15
  15.0 0.8 compare_convert_fusion
  15.8 1.2 fusion.18
  16.9 1.2 fusion.19
  18.1 0.6 copy-done.1
  18.8 0.6 fusion.161
  19.4 0.6 broadcast_multiply_fusion.6
  19.9 1.2 fusion.6
  21.1 1.2 fusion.7
  22.4 0.7 fusion.73
  23.3 1.2 reshape.107
  24.8 1.2 reshape.105
  26.6 10.7 %all-to-all-start.1 = ((f32[32,1,2048]{2,1,0:T(1,128)}), f32[32,1,2048]{2,1,0:T(1,128)S(1)}, u32[]{:S(2)}, u32[]{:S(2)}) async-start(f32[32,1,2048]{2,1,0:T(1,128)} %reshape.107), calls=%async_computation.1 | async-start | bytes 524288 | tf_op jit(solution)/shard_map/all_to_all | solution.py:84
  37.6 11.1 %all-to-all-done.1 = f32[32,1,2048]{2,1,0:T(1,128)S(1)} async-done(((f32[32,1,2048]{2,1,0:T(1,128)}), f32[32,1,2048]{2,1,0:T(1,128)S(1)}, u32[]{:S(2)}, u32[]{:S(2)}) %all-to-all-start.1) | async-done | bytes 262176 | tf_op jit(solution)/shard_map/all_to_all | solution.py:84
  48.7 4.9 %all-to-all-start = ((f32[32,1,2048]{2,1,0:T(1,128)}), f32[32,1,2048]{2,1,0:T(1,128)S(1)}, u32[]{:S(2)}, u32[]{:S(2)}) async-start(f32[32,1,2048]{2,1,0:T(1,128)} %reshape.105), calls=%async_computation | async-start | bytes 524288 | tf_op jit(solution)/shard_map/all_to_all | solution.py:83
  54.6 1.2 reduce.1
  56.6 8.3 %all-to-all-done = f32[32,1,2048]{2,1,0:T(1,128)S(1)} async-done(((f32[32,1,2048]{2,1,0:T(1,128)}), f32[32,1,2048]{2,1,0:T(1,128)S(1)}, u32[]{:S(2)}, u32[]{:S(2)}) %all-to-all-start) | async-done | bytes 262176 | tf_op jit(solution)/shard_map/all_to_all | solution.py:83
  64.9 1.2 reduce
  68.6 0.9 fusion.43
  69.5 0.9 fusion.51
  70.9 0.9 fusion.5
  71.8 0.9 fusion.40
  72.7 0.9 fusion.32
  73.5 0.9 fusion.3
  74.4 0.9 fusion
  75.3 1.1 fusion.1
  76.4 0.8 fusion.69
  77.2 0.8 convolution_subtract_fusion.5
  78.2 1.2 reshape.109
  79.4 4.7 %all-to-all-start.3 = ((f32[32,1,2048]{2,1,0:T(1,128)}), f32[32,1,2048]{2,1,0:T(1,128)S(1)}, u32[]{:S(2)}, u32[]{:S(2)}) async-start(f32[32,1,2048]{2,1,0:T(1,128)} %reshape.109), calls=%async_computation.3 | async-start | bytes 524288 | tf_op jit(solution)/shard_map/all_to_all | solution.py:92
  84.2 0.6 broadcast_multiply_fusion.5
  84.8 0.8 fusion.68
  85.5 0.8 convolution_add_fusion.5
  86.6 1.2 %reshape.111 = f32[32,1,2048]{2,1,0:T(1,128)} reshape(f32[128,2,4,64]{3,2,1,0:T(4,128)S(1)} %bitcast.172) | data formatting | bytes 524288
  87.8 7.9 %all-to-all-done.3 = f32[32,1,2048]{2,1,0:T(1,128)S(1)} async-done(((f32[32,1,2048]{2,1,0:T(1,128)}), f32[32,1,2048]{2,1,0:T(1,128)S(1)}, u32[]{:S(2)}, u32[]{:S(2)}) %all-to-all-start.3) | async-done | bytes 262176 | tf_op jit(solution)/shard_map/all_to_all | solution.py:92
  95.7 4.7 %all-to-all-start.4 = ((f32[32,1,2048]{2,1,0:T(1,128)}), f32[32,1,2048]{2,1,0:T(1,128)S(1)}, u32[]{:S(2)}, u32[]{:S(2)}) async-start(f32[32,1,2048]{2,1,0:T(1,128)} %reshape.111), calls=%async_computation.4 | async-start | bytes 524288 | tf_op jit(solution)/shard_map/all_to_all | solution.py:93
  100.4 0.8 add_multiply_fusion
  102.7 1.2 reduce.2
  104.7 1.0 fusion.37
  105.7 1.0 fusion.35
  106.7 5.2 %all-to-all-done.4 = f32[32,1,2048]{2,1,0:T(1,128)S(1)} async-done(((f32[32,1,2048]{2,1,0:T(1,128)}), f32[32,1,2048]{2,1,0:T(1,128)S(1)}, u32[]{:S(2)}, u32[]{:S(2)}) %all-to-all-start.4) | async-done | bytes 262176 | tf_op jit(solution)/shard_map/all_to_all | solution.py:93
  111.9 1.2 reduce.3
  113.9 1.0 fusion.8
  114.9 1.0 fusion.9
  116.8 1.8 %fusion.13 = (f32[1,2,4,128,128]{4,3,2,1,0:T(8,128)S(1)}, f32[1,2,4,128,128]{4,3,2,1,0:T(8,128)S(1)}) fusion(f32[1,2,4,128,32]{4,3,2,1,0:T(8,128)S(1)} %copy.148, f32[1,2,4,128,32]{4,3,2,1,0:T(8,128)S(1)} %copy.147, f32[2,2,4,128,128]{4,3,2,1,0:T(8,128)} %param.8, f32[2,2,4,128,128]{4,3,2,1,0:T(8,128)S(1)} %copy-done, f32[128]{0:T(128)S(1)} %pad.6.clone, ...), kind=kLoop, calls=%fused_computation.27 | loop fusion | flops 2621440 | bytes 4194824 | tf_op jit(solution)/shard_map/mul | solution.py:117
  118.6 1.0 pad_maximum_fusion
  (48 shorter events, 9.2 us)
Async XLA Ops:
  0.0 15.8 %copy-start = (f32[2,2,4,128,128]{4,3,2,1,0:T(8,128)S(1)}, f32[2,2,4,128,128]{4,3,2,1,0:T(8,128)}, u32[]{:S(2)}) copy-start(f32[2,2,4,128,128]{4,3,2,1,0:T(8,128)} %param.7) | copy-start | bytes 3145732
  1.6 25.0 %all-to-all-start.2 = ((f32[16,8,4,128]{3,1,2,0:T(8,128)}), f32[16,8,4,128]{3,1,2,0:T(8,128)S(1)}, u32[]{:S(2)}, u32[]{:S(2)}) async-start(f32[16,8,4,128]{3,1,2,0:T(8,128)} %broadcast_in_dim.4), calls=%async_computation.2 | async-start | bytes 524288 | tf_op jit(solution)/shard_map/all_to_all | solution.py:15
  18.1 0.7 copy-start.1
  26.6 22.1 %all-to-all-start.1 = ((f32[32,1,2048]{2,1,0:T(1,128)}), f32[32,1,2048]{2,1,0:T(1,128)S(1)}, u32[]{:S(2)}, u32[]{:S(2)}) async-start(f32[32,1,2048]{2,1,0:T(1,128)} %reshape.107), calls=%async_computation.1 | async-start | bytes 524288 | tf_op jit(solution)/shard_map/all_to_all | solution.py:84
  48.7 16.2 %all-to-all-start = ((f32[32,1,2048]{2,1,0:T(1,128)}), f32[32,1,2048]{2,1,0:T(1,128)S(1)}, u32[]{:S(2)}, u32[]{:S(2)}) async-start(f32[32,1,2048]{2,1,0:T(1,128)} %reshape.105), calls=%async_computation | async-start | bytes 524288 | tf_op jit(solution)/shard_map/all_to_all | solution.py:83
  79.4 16.2 %all-to-all-start.3 = ((f32[32,1,2048]{2,1,0:T(1,128)}), f32[32,1,2048]{2,1,0:T(1,128)S(1)}, u32[]{:S(2)}, u32[]{:S(2)}) async-start(f32[32,1,2048]{2,1,0:T(1,128)} %reshape.109), calls=%async_computation.3 | async-start | bytes 524288 | tf_op jit(solution)/shard_map/all_to_all | solution.py:92
  95.7 16.2 %all-to-all-start.4 = ((f32[32,1,2048]{2,1,0:T(1,128)}), f32[32,1,2048]{2,1,0:T(1,128)S(1)}, u32[]{:S(2)}, u32[]{:S(2)}) async-start(f32[32,1,2048]{2,1,0:T(1,128)} %reshape.111), calls=%async_computation.4 | async-start | bytes 524288 | tf_op jit(solution)/shard_map/all_to_all | solution.py:93
where the time goes:
time: 120 us
  starting transfers between devices  38.5 us (32%)
  waiting for transfers between devices  32.5 us (27%)
  matrix products  21.2 us (18%)
  local copies, waits for them, and re-layouts  13.4 us (11%)
  other arithmetic  12.2 us (10%)
  between operations  1.9 us (2%)
    all_to_all x1, starting transfers between devices, from_everyone(): return lax.all_to_all(copies, axis, split_axis=0, concat_axis=0, tiled=True)  13.4 us
    all_to_all x1, waiting for transfers between devices, local(): lax.all_to_all(imag_part, 'fft', split_axis=2, concat_axis=1, tiled=True)  11.1 us
    all_to_all x1, starting transfers between devices, local(): lax.all_to_all(imag_part, 'fft', split_axis=2, concat_axis=1, tiled=True)  10.7 us
    all_to_all x1, waiting for transfers between devices, local(): lax.all_to_all(real_part, 'fft', split_axis=2, concat_axis=1, tiled=True)  8.32 us
    all_to_all x1, waiting for transfers between devices, local(): lax.all_to_all(real_part, 'fft', split_axis=1, concat_axis=2, tiled=True)  7.87 us
    unnamed x13, local copies, waits for them, and re-layouts  7.61 us
    dot_general x6, matrix products, transform(): imag_sin = jnp.einsum(form, imag_part, sine_table, precision=highest)  5.5 us
    dot_general x6, matrix products, transform(): imag_cos = jnp.einsum(form, imag_part, cosine_table, precision=highest)  5.27 us
  transfers between devices with their start and end apart: 5, of which 4 were waited for; matrix products, arithmetic and copies ran while one was open for 19% of the time, Pallas kernels for 0%

commit v1 on v0

v1 whole, which is shorter than its diff:
```python
import functools
import math

import jax
import jax.numpy as jnp
import numpy as np
from jax import lax
from jax.experimental import pallas as pl
from jax.experimental.pallas import tpu as pltpu
from jax.sharding import PartitionSpec as P

N = 128
KEPT = 64
HALF = KEPT // 2
FFT = 32
ACTIVE = 16
BANDS = 2
MESH = pl.DeviceIdType.MESH


def kept_indices():
    return np.concatenate([np.arange(HALF), np.arange(N - HALF, N)])


def cos_sin(rows, cols):
    angles = (np.outer(rows, cols) % N) * (2.0 * math.pi / N)
    return np.cos(angles), np.sin(angles)


def split(table):
    high = table.astype(jnp.bfloat16)
    low = (table - high.astype(np.float64)).astype(jnp.bfloat16)
    return high, low


def stacked(cosine, sine):
    cos_high, cos_low = split(cosine)
    sin_high, sin_low = split(sine)
    zero = np.zeros_like(cos_low)
    return np.concatenate(
        [
            np.concatenate([cos_high, cos_high], axis=1),
            np.concatenate([sin_high, sin_high], axis=1),
            np.concatenate([cos_low, zero], axis=1),
            np.concatenate([sin_low, zero], axis=1),
        ],
        axis=0,
    )


def make_tables():
    grid = np.arange(N)
    kept = kept_indices()
    slots = np.arange(ACTIVE)
    first_gx = 4 * np.where(slots < ACTIVE // 2, slots, slots + FFT - ACTIVE)

    cosine, sine = cos_sin(grid, kept)
    base = np.concatenate([cosine, sine], axis=1).reshape(FFT, 4, 2 * KEPT)
    full = np.zeros((FFT, 2, 4, 2, 2 * KEPT))
    for q in range(2):
        full[:, q, :, q, :] = base
    inverse_z = np.concatenate(split(full.reshape(2 * N, 2 * N)), axis=1)

    lanes = np.arange(N)
    natural = (lanes < HALF) | (lanes >= N - HALF)
    gy = np.where(natural, lanes, (lanes + KEPT) % N)
    cosine, sine = cos_sin(gy, grid)
    pick = natural[:, None]
    table = np.concatenate([np.where(pick, cosine, -sine), np.where(pick, sine, cosine)], axis=1)
    high, low = split(table)
    inverse_y = np.concatenate([high, high, low], axis=0)

    order = (first_gx[None, :, None] + 2 * np.arange(2)[:, None, None] + np.arange(2)[None, None, :]).reshape(-1)
    cosine, sine = cos_sin(grid, order)
    cos_high, cos_low = split(cosine)
    sin_high, sin_low = split(sine)
    zero = np.zeros_like(cos_low)
    inverse_x = np.concatenate(
        [
            np.concatenate([cos_high, sin_high, cos_high, sin_high], axis=1),
            np.concatenate([cos_low, sin_low, zero, zero], axis=1),
        ],
        axis=0,
    )

    order = (np.arange(4)[:, None] + first_gx[None, :]).reshape(-1)
    cosine, sine = cos_sin(order, grid)
    forward_x = stacked(cosine / N, sine / N)

    cosine, sine = cos_sin(grid, gy)
    pick = natural[None, :]
    table = np.concatenate([np.where(pick, cosine, -sine), np.where(pick, sine, cosine)], axis=0) / N
    forward_y = np.concatenate(split(table), axis=1)

    cosine, sine = cos_sin(kept, grid)
    forward_z = stacked(cosine / N, sine / N)
    return [inverse_z, inverse_y, inverse_x, forward_x, forward_y, forward_z]


def halves(value):
    high = value.astype(jnp.bfloat16)
    low = (value - high.astype(jnp.float32)).astype(jnp.bfloat16)
    return high, low


def dot(left, right):
    return jnp.dot(left, right, preferred_element_type=jnp.float32)


def kernel(
    wave,
    previous,
    potential,
    extent,
    metric,
    center,
    halfwidth,
    iz_hbm,
    iy_hbm,
    ix_hbm,
    fx_hbm,
    fy_hbm,
    fz_hbm,
    out,
    wbuf,
    pbuf,
    vbuf,
    iz,
    iy,
    ix,
    fx,
    fy,
    fz,
    zhigh,
    zlow,
    sbuf,
    rbuf,
    yre,
    yim,
    qhigh,
    qlow,
    gbuf,
    hbuf,
    obuf,
    wsem,
    psem,
    tsem,
    lsem,
    osem,
    fsend,
    frecv,
    gsend,
    grecv,
    vsend,
    vrecv,
):
    me = lax.axis_index("fft")
    band = lax.axis_index("band")
    my_x, my_z = band // 4, band % 4
    active = jnp.logical_or(me < ACTIVE // 2, me >= FFT - ACTIVE // 2)
    slot = jnp.where(me < ACTIVE // 2, me, me - (FFT - ACTIVE))

    def peer_at(step):
        spot = step + jnp.where(step >= 28, 1, 0)
        k, i = spot // 4, spot % 4
        dy = 4 + (1 - 2 * (k % 2)) * ((k + 1) // 2)
        return ((me // 4 + dy) % 8) * 4 + (me + i) % 4

    load_v = pltpu.make_async_copy(potential, vbuf.at[pl.ds(pl.multiple_of(band * 32, 32), 32), :], lsem)
    load_v.start()
    table_refs = ((iz_hbm, iz), (iy_hbm, iy), (ix_hbm, ix), (fx_hbm, fx), (fy_hbm, fy), (fz_hbm, fz))
    table_copies = [pltpu.make_async_copy(a, b, tsem.at[i]) for i, (a, b) in enumerate(table_refs)]

    def wave_copies(b):
        return [
            pltpu.make_async_copy(
                wave.at[:, b, :, pl.ds(h * (N - HALF), HALF), :],
                wbuf.at[:, b, :, pl.ds(h * HALF, HALF), :],
                wsem.at[b, h],
            )
            for h in range(2)
        ]

    def previous_copies():
        return [
            pltpu.make_async_copy(
                previous.at[:, :, :, pl.ds(h * (N - HALF), HALF), :],
                pbuf.at[:, :, :, pl.ds(h * HALF, HALF), :],
                psem.at[h],
            )
            for h in range(2)
        ]

    @pl.when(active)
    def _():
        for b in range(BANDS):
            for copy in wave_copies(b):
                copy.start()

    for copy in table_copies:
        copy.start()

    barrier = pltpu.get_barrier_semaphore()

    def greet(step, carry):
        pl.semaphore_signal(barrier, inc=1, device_id={"fft": peer_at(step)}, device_id_type=MESH)
        return carry

    lax.fori_loop(0, FFT - 1, greet, 0)
    z_peers = [my_x * 4 + (my_z + d) % 4 for d in (2, 1, 3)]
    x_peers = [((my_x + d) % 4) * 4 + my_z for d in (2, 1, 3)]
    for peer in z_peers + x_peers:
        pl.semaphore_signal(barrier, inc=1, device_id={"band": peer}, device_id_type=MESH)

    @pl.when(active)
    def _():
        for copy in previous_copies():
            copy.start()

    row = lax.broadcasted_iota(jnp.int32, (KEPT, N), 0)
    lane = lax.broadcasted_iota(jnp.int32, (KEPT, N), 1)
    signed_gz = jnp.where(row < HALF, row, row - KEPT)
    signed_gy = jnp.where(lane < N // 2, lane, lane - N)
    turn = jnp.where(jnp.logical_or(lane < HALF, lane >= N - HALF), -1.0, 1.0).astype(jnp.float32)

    def keep_of(j):
        return (jnp.abs(signed_gz) <= extent[pl.ds(j, 1), :]).astype(jnp.float32)

    def to_planes(b):
        for copy in wave_copies(b):
            copy.wait()
        for p in range(2):
            for q in range(2):
                j = 2 * p + q
                keep = keep_of(j)
                packed = keep * wbuf[0, b, j] + pltpu.roll(keep * wbuf[1, b, j], KEPT, axis=1)
                turned = pltpu.roll(packed, KEPT, axis=1) * turn
                for t, part in enumerate((packed, turned)):
                    high, low = halves(part)
                    rows = slice((2 * q + t) * KEPT, (2 * q + t + 1) * KEPT)
                    zhigh[rows, p * N : (p + 1) * N] = high
                    zlow[rows, p * N : (p + 1) * N] = low
        sbuf[b] = (
            dot(iz[:, : 2 * N], zhigh[...]) + dot(iz[:, 2 * N :], zhigh[...]) + dot(iz[:, : 2 * N], zlow[...])
        )
        mine = sbuf[b, pl.ds(pl.multiple_of(me * 8, 8), 8), :]
        rbuf[b, pl.ds(pl.multiple_of(slot * 8, 8), 8), :] = mine

    def plane_copy(b, peer):
        return pltpu.make_async_remote_copy(
            src_ref=sbuf.at[b, pl.ds(pl.multiple_of(peer * 8, 8), 8), :],
            dst_ref=rbuf.at[b, pl.ds(pl.multiple_of(slot * 8, 8), 8), :],
            send_sem=fsend.at[b],
            recv_sem=frecv.at[b],
            device_id={"fft": peer},
            device_id_type=MESH,
        )

    def send_planes(b):
        def step(n, carry):
            plane_copy(b, peer_at(n)).start()
            return carry

        lax.fori_loop(0, FFT - 1, step, 0)

    def column_copy(b, peer):
        where = jnp.where(peer < ACTIVE // 2, peer, peer - (FFT - ACTIVE))
        return pltpu.make_async_remote_copy(
            src_ref=gbuf.at[b, pl.ds(pl.multiple_of(where * 16, 16), 16), :],
            dst_ref=hbuf.at[b, pl.ds(pl.multiple_of(me * 16, 16), 16), :],
            send_sem=gsend.at[b],
            recv_sem=grecv.at[b],
            device_id={"fft": peer},
            device_id_type=MESH,
        )

    def send_columns(b):
        def step(n, carry):
            peer = peer_at(n)

            @pl.when(jnp.logical_or(peer < ACTIVE // 2, peer >= FFT - ACTIVE // 2))
            def _():
                column_copy(b, peer).start()

            return carry

        lax.fori_loop(0, FFT - 1, step, 0)

    def awaited(ref, send, recv):
        return pltpu.make_async_remote_copy(
            src_ref=ref, dst_ref=ref, send_sem=send, recv_sem=recv, device_id={"fft": me}, device_id_type=MESH
        )

    def v_copy(start, rows, phase, peer):
        where = vbuf.at[pl.ds(pl.multiple_of(start, 32), rows), :]
        return pltpu.make_async_remote_copy(
            src_ref=where,
            dst_ref=where,
            send_sem=vsend.at[phase],
            recv_sem=vrecv.at[phase],
            device_id={"band": peer},
            device_id_type=MESH,
        )

    @pl.when(active)
    def _():
        table_copies[0].wait()
        to_planes(0)

    load_v.wait()
    pl.semaphore_wait(barrier, FFT - 1 + 6)

    for peer in z_peers:
        v_copy(band * 32, 32, 0, peer).start()

    @pl.when(active)
    def _():
        send_planes(0)
        to_planes(1)
        send_planes(1)
        obuf[...] = jnp.zeros_like(obuf)

    @pl.when(jnp.logical_not(active))
    def _():
        table_copies[0].wait()
        obuf[...] = jnp.zeros_like(obuf)
        for b in range(BANDS):
            pltpu.make_async_copy(obuf.at[:, b], out.at[:, b], osem.at[b]).start()

    awaited(vbuf.at[pl.ds(0, 96), :], vsend.at[0], vrecv.at[0]).wait_recv()
    for peer in x_peers:
        v_copy(my_x * 128, 128, 1, peer).start()

    for copy in table_copies[1:5]:
        copy.wait()

    for b in range(BANDS):

        @pl.when(active)
        def _():
            awaited(rbuf.at[b, pl.ds(0, 8 * (ACTIVE - 1)), :], fsend.at[b], frecv.at[b]).wait_recv()

        @pl.when(jnp.logical_not(active))
        def _():
            awaited(rbuf.at[b], fsend.at[b], frecv.at[b]).wait_recv()

        for p in range(2):
            high, low = halves(rbuf[b, :, p * N : (p + 1) * N])
            plane = dot(jnp.concatenate([high, low, high], axis=1), iy[...])
            yre[p * N : (p + 1) * N, :] = plane[:, :N]
            yim[p * N : (p + 1) * N, :] = plane[:, N:]
        if b == 0:
            awaited(vbuf.at[pl.ds(0, 384), :], vsend.at[1], vrecv.at[1]).wait_recv()
        for z in range(4):
            rh, rl = halves(yre[pl.ds(z, KEPT, stride=4), :])
            ih, il = halves(yim[pl.ds(z, KEPT, stride=4), :])
            right = jnp.concatenate(
                [
                    jnp.concatenate([rh, ih], axis=1),
                    jnp.concatenate([-ih, rh], axis=1),
                    jnp.concatenate([rl, il], axis=1),
                    jnp.concatenate([-il, rl], axis=1),
                ],
                axis=0,
            )
            field = dot(ix[...], right)
            field = field[:N] + field[N:]
            local_v = vbuf[pl.ds(z, N, stride=4), :]
            rh, rl = halves(field[:, :N] * local_v)
            ih, il = halves(field[:, N:] * local_v)
            right = jnp.concatenate(
                [jnp.concatenate([rh, ih], axis=1), jnp.concatenate([rl, il], axis=1)], axis=0
            )
            both = dot(fx[...], right)
            both = both[:N] + both[N:]
            cos_part, sin_part = both[:KEPT], both[KEPT:]
            high, low = halves(cos_part[:, :N] + sin_part[:, N:])
            qhigh[z * KEPT : (z + 1) * KEPT, :N] = high
            qlow[z * KEPT : (z + 1) * KEPT, :N] = low
            high, low = halves(cos_part[:, N:] - sin_part[:, :N])
            qhigh[z * KEPT : (z + 1) * KEPT, N:] = high
            qlow[z * KEPT : (z + 1) * KEPT, N:] = low
        wide = dot(qhigh[...], fy[...])
        packed = wide[:, :N] + wide[:, N:] + dot(qlow[...], fy[:, :N])
        for z in range(4):
            for j in range(4):
                gbuf[b, pl.ds(z * 4 + j, ACTIVE, stride=16), :] = packed[
                    z * KEPT + j * ACTIVE : z * KEPT + (j + 1) * ACTIVE
                ]

        @pl.when(active)
        def _():
            mine = gbuf[b, pl.ds(pl.multiple_of(slot * 16, 16), 16), :]
            hbuf[b, pl.ds(pl.multiple_of(me * 16, 16), 16), :] = mine

        send_columns(b)

    table_copies[5].wait()

    @pl.when(active)
    def _():
        for copy in previous_copies():
            copy.wait()
        step_z = (2.0 * math.pi / N) * signed_gz.astype(jnp.float32)
        step_y = (2.0 * math.pi / N) * signed_gy.astype(jnp.float32)
        plane_kinetic = metric[2] * (step_z * step_z) + metric[1] * (step_y * step_y)
        factor = jnp.full((1, 1), 2.0, jnp.float32) / jnp.full((1, 1), halfwidth[0], jnp.float32)
        middle = center[0]
        for b in range(BANDS):
            awaited(hbuf.at[b, pl.ds(0, 16 * (FFT - 1)), :], gsend.at[b], grecv.at[b]).wait_recv()
            for p in range(2):
                h0, l0 = halves(hbuf[b, pl.ds(2 * p, N, stride=4), :])
                h1, l1 = halves(hbuf[b, pl.ds(2 * p + 1, N, stride=4), :])
                right = jnp.concatenate(
                    [jnp.concatenate([h0, h1], axis=1), jnp.concatenate([l0, l1], axis=1)], axis=0
                )
                both = dot(fz[...], right)
                both = both[:N] + both[N:]
                for q in range(2):
                    j = 2 * p + q
                    cos_part = both[:KEPT, q * N : (q + 1) * N]
                    sin_part = both[KEPT:, q * N : (q + 1) * N]
                    applied = cos_part - turn * pltpu.roll(sin_part, KEPT, axis=1)
                    keep = keep_of(j)
                    gx = me * 4 + j
                    signed_gx = jnp.where(gx < N // 2, gx, gx - N).astype(jnp.float32)
                    step_x = (2.0 * math.pi / N) * signed_gx
                    kinetic = 0.5 * (metric[0] * (step_x * step_x) + plane_kinetic)
                    for t, term in enumerate((applied, pltpu.roll(applied, KEPT, axis=1))):
                        coefficient = keep * wbuf[t, b, j]
                        result = keep * (
                            factor * (kinetic * coefficient + term - middle * coefficient) - pbuf[t, b, j]
                        )
                        obuf[t, b, j, :HALF, :] = result[:HALF]
                        obuf[t, b, j, N - HALF :, :] = result[HALF:]
            pltpu.make_async_copy(obuf.at[:, b], out.at[:, b], osem.at[b]).start()

    @pl.when(active)
    def _():
        for b in range(BANDS):
            awaited(sbuf.at[b, pl.ds(0, 8 * (FFT - 1)), :], fsend.at[b], frecv.at[b]).wait_send()
            awaited(gbuf.at[b, pl.ds(0, 16 * (ACTIVE - 1)), :], gsend.at[b], grecv.at[b]).wait_send()

    @pl.when(jnp.logical_not(active))
    def _():
        for b in range(BANDS):
            awaited(gbuf.at[b], gsend.at[b], grecv.at[b]).wait_send()

    awaited(vbuf.at[pl.ds(0, 96), :], vsend.at[0], vrecv.at[0]).wait_send()
    awaited(vbuf.at[pl.ds(0, 384), :], vsend.at[1], vrecv.at[1]).wait_send()
    for b in range(BANDS):
        pltpu.make_async_copy(obuf.at[:, b], out.at[:, b], osem.at[b]).wait()


def local(tables, wave, previous, potential, column_extent, metric, center, halfwidth):
    any_spec = pl.BlockSpec(memory_space=pl.ANY)
    vmem_spec = pl.BlockSpec(memory_space=pltpu.VMEM)
    smem_spec = pl.BlockSpec(memory_space=pltpu.SMEM)
    f32, bf16 = jnp.float32, jnp.bfloat16
    dma = pltpu.SemaphoreType.DMA
    return pl.pallas_call(
        kernel,
        out_shape=jax.ShapeDtypeStruct(wave.shape, f32),
        in_specs=[any_spec, any_spec, any_spec, vmem_spec, smem_spec, smem_spec, smem_spec] + [any_spec] * 6,
        out_specs=any_spec,
        scratch_shapes=[
            pltpu.VMEM((2, BANDS, 4, KEPT, N), f32),
            pltpu.VMEM((2, BANDS, 4, KEPT, N), f32),
            pltpu.VMEM((4 * N, N), f32),
            *[pltpu.VMEM(table.shape, bf16) for table in tables],
            pltpu.VMEM((2 * N, 2 * N), bf16),
            pltpu.VMEM((2 * N, 2 * N), bf16),
            pltpu.VMEM((BANDS, 2 * N, 2 * N), f32),
            pltpu.VMEM((BANDS, N, 2 * N), f32),
            pltpu.VMEM((2 * N, N), f32),
            pltpu.VMEM((2 * N, N), f32),
            pltpu.VMEM((2 * N, 2 * N), bf16),
            pltpu.VMEM((2 * N, 2 * N), bf16),
            pltpu.VMEM((BANDS, 2 * N, N), f32),
            pltpu.VMEM((BANDS, 4 * N, N), f32),
            pltpu.VMEM((2, BANDS, 4, N, N), f32),
            dma((BANDS, 2)),
            dma((2,)),
            dma((6,)),
            dma,
            dma((BANDS,)),
            dma((BANDS,)),
            dma((BANDS,)),
            dma((BANDS,)),
            dma((BANDS,)),
            dma((2,)),
            dma((2,)),
        ],
        compiler_params=pltpu.CompilerParams(collective_id=0, has_side_effects=True),
    )(wave, previous, potential.reshape(32, N), column_extent, metric, center, halfwidth, *tables)


def solution(mesh):
    tables = [jnp.asarray(table) for table in make_tables()]
    in_specs = (
        P(None, "band", "fft", None, None),
        P(None, "band", "fft", None, None),
        P("band", "fft", None),
        P("fft", None),
        P(),
        P(),
        P(),
    )
    out_specs = P(None, "band", "fft", None, None)
    return jax.shard_map(
        functools.partial(local, tables), mesh=mesh, in_specs=in_specs, out_specs=out_specs, check_vma=False
    )
```

time: 120 us -> 44.8 us (0.37)
  Pallas kernels: 0 us -> 41 us
  starting transfers between devices: 38.5 us -> 0 us
  waiting for transfers between devices: 32.5 us -> 0 us
  matrix products: 21.2 us -> 0 us
  other arithmetic: 12.2 us -> 0 us
  local copies, waits for them, and re-layouts: 13.4 us -> 2.3 us
    pallas_call x0 -> x1, Pallas kernels: none -> 41 us  [local(): pl.pallas_call(kernel, out_shape=jax.ShapeDtypeStruct(wave.shape, f32), i...]
    all_to_all x5 -> x0, starting transfers between devices: 38.5 us -> none  [the longest x1 13.4 us: from_everyone(): return lax.all_to_all(copies, axis, split_axis=0, concat_axis=0, tiled=True)]
    all_to_all x5 -> x0, waiting for transfers between devices: 32.5 us -> none  [the longest x1 11.1 us: local(): lax.all_to_all(imag_part, 'fft', split_axis=2, concat_axis=1, tiled=True)]
    dot_general x24 -> x0, matrix products: 21.2 us -> none  [the longest x6 5.5 us: transform(): imag_sin = jnp.einsum(form, imag_part, sine_table, precision=highest)]
    unnamed x13 -> x1, local copies, waits for them, and re-layouts: 7.61 us -> 2.3 us
    all_to_all x4 -> x0, other arithmetic: 4.73 us -> none  [the longest x1 1.18 us: local(): lax.all_to_all(real_part, 'fft', split_axis=2, concat_axis=1, tiled=True)]
    mul x5 -> x0, other arithmetic: 4.46 us -> none  [the longest x1 1.81 us: local(): keep_mask * (factor * (kinetic * coeff_real + real_part - center[0] * coe...]
    all_to_all x10 -> x0, local copies, waits for them, and re-layouts: 2.32 us -> none  [the longest x3 0.96 us: local(): lax.all_to_all(real_part, 'fft', split_axis=2, concat_axis=1, tiled=True)]
  transfers between devices with their start and end apart: 5 -> 0, of which waited for: 4 -> 0; matrix products, arithmetic and copies ran while one was open for 19% -> 0% of each run, Pallas kernels for 0% -> 0%
where the time goes in v1:
time: 44.8 us; the launch traced here: 44.6 us
  Pallas kernels  41 us (92%)
  local copies, waits for them, and re-layouts  2.3 us (5%)
  between operations  1.3 us (3%)
    pallas_call x1, Pallas kernels, local(): pl.pallas_call(kernel, out_shape=jax.ShapeDtypeStruct(wave.shape, f32), i...  41 us
    unnamed x1, local copies, waits for them, and re-layouts  2.3 us

profile of v1, /device:TPU:1, one launch (start us, length us, event | category | flops | bytes accessed | tf_op | source)
XLA Modules:
  0.0 44.6 jit_solution(18043767404377634000)
XLA Ops:
  1.3 41.0 %shard_map.127 = f32[2,2,4,128,128]{4,3,2,1,0:T(8,128)} custom-call(f32[2,2,4,128,128]{4,3,2,1,0:T(8,128)} %wave.1, f32[2,2,4,128,128]{4,3,2,1,0:T(8,128)} %previous.1, f32[32,128]{1,0:T(8,128)} %bitcast.1, s32[4,128]{1,0:T(4,128)} %extent.1, f32[3]{0:T(128)} %metric.1, f32[1]{0:T(128)S(6)} %copy.15.center, f32[1]{0:T(128)S(6)} %copy.16.halfwidth, ...), custom_call_target="tpu_custom_call" | custom-call | tf_op jit(solution)/shard_map/pallas_call | solution.py:461
  42.3 2.3 %copy.17 = f32[2,2,4,128,128]{4,3,2,1,0:T(8,128)} copy(f32[2,2,4,128,128]{4,3,2,1,0:T(8,128)} %shard_map.127) | data formatting | bytes 2097152

commit v2 on v1

v2 whole, which is shorter than its diff:
```python
import functools
import math

import jax
import jax.numpy as jnp
import numpy as np
from jax import lax
from jax.experimental import pallas as pl
from jax.experimental.pallas import tpu as pltpu
from jax.sharding import PartitionSpec as P

N = 128
KEPT = 64
HALF = KEPT // 2
FFT = 32
ACTIVE = 16
BANDS = 2
PLANES = 5
FEW = 3
MESH = pl.DeviceIdType.MESH


def kept_indices():
    return np.concatenate([np.arange(HALF), np.arange(N - HALF, N)])


def cos_sin(rows, cols):
    angles = (np.outer(rows, cols) % N) * (2.0 * math.pi / N)
    return np.cos(angles), np.sin(angles)


def split(table):
    high = table.astype(jnp.bfloat16)
    low = (table - high.astype(np.float64)).astype(jnp.bfloat16)
    return high, low


def stacked(cosine, sine):
    cos_high, cos_low = split(cosine)
    sin_high, sin_low = split(sine)
    zero = np.zeros_like(cos_low)
    return np.concatenate(
        [
            np.concatenate([cos_high, cos_high], axis=1),
            np.concatenate([sin_high, sin_high], axis=1),
            np.concatenate([cos_low, zero], axis=1),
            np.concatenate([sin_low, zero], axis=1),
        ],
        axis=0,
    )


def make_tables():
    grid = np.arange(N)
    kept = kept_indices()
    slots = np.arange(ACTIVE)
    first_gx = 4 * np.where(slots < ACTIVE // 2, slots, slots + FFT - ACTIVE)

    cosine, sine = cos_sin(grid, kept)
    high, low = split(np.concatenate([cosine, sine], axis=1))
    zero = np.zeros_like(low)
    inverse_z = np.concatenate([np.concatenate([high, high], axis=1), np.concatenate([low, zero], axis=1)], axis=0)

    lanes = np.arange(N)
    natural = (lanes < HALF) | (lanes >= N - HALF)
    gy = np.where(natural, lanes, (lanes + KEPT) % N)
    cosine, sine = cos_sin(gy, grid)
    pick = natural[:, None]
    table = np.concatenate([np.where(pick, cosine, -sine), np.where(pick, sine, cosine)], axis=1)
    high, low = split(table)
    inverse_y = np.concatenate([high, high, low], axis=0)

    order = (first_gx[:, None] + np.arange(4)[None, :]).reshape(-1)
    cosine, sine = cos_sin(grid, order)
    cos_high, cos_low = split(cosine)
    sin_high, sin_low = split(sine)
    zero = np.zeros_like(cos_low)
    inverse_x = np.concatenate(
        [
            np.concatenate([cos_high, sin_high, cos_high, sin_high], axis=1),
            np.concatenate([cos_low, sin_low, zero, zero], axis=1),
        ],
        axis=0,
    )

    cosine, sine = cos_sin(order, grid)
    forward_x = stacked(cosine / N, sine / N)

    cosine, sine = cos_sin(grid, gy)
    pick = natural[None, :]
    table = np.concatenate([np.where(pick, cosine, -sine), np.where(pick, sine, cosine)], axis=0) / N
    forward_y = np.concatenate(split(table), axis=1)

    cosine, sine = cos_sin(kept, grid)
    forward_z = stacked(cosine / N, sine / N)
    return [inverse_z, inverse_y, inverse_x, forward_x, forward_y, forward_z]


def halves(value):
    high = value.astype(jnp.bfloat16)
    low = (value - high.astype(jnp.float32)).astype(jnp.bfloat16)
    return high, low


def dot(left, right):
    return jnp.dot(left, right, preferred_element_type=jnp.float32)


def kernel(
    wave,
    previous,
    potential,
    extent_hbm,
    metric_hbm,
    center,
    halfwidth,
    iz_hbm,
    iy_hbm,
    ix_hbm,
    fx_hbm,
    fy_hbm,
    fz_hbm,
    out,
    extent,
    metric,
    wbuf,
    pbuf,
    vbuf,
    iz,
    iy,
    ix,
    fx,
    fy,
    fz,
    vown,
    zboth,
    sbuf,
    rbuf,
    yre,
    yim,
    qhigh,
    qlow,
    gbuf,
    hbuf,
    base,
    wsem,
    psem,
    tsem,
    lsem,
    fsend,
    frecv,
    gsend,
    grecv,
    vsend,
    vrecv,
    esend,
    erecv,
    ready,
):
    me = lax.axis_index("fft")
    band = lax.axis_index("band")
    my_x, my_z = lax.div(band, 4), lax.rem(band, 4)
    my_y, my_low = lax.div(me, 4), lax.rem(me, 4)
    active = jnp.logical_or(me < ACTIVE // 2, me >= FFT - ACTIVE // 2)
    slot = jnp.where(me < ACTIVE // 2, me, me - (FFT - ACTIVE))
    lows = [my_low] + [lax.rem(my_low + i, 4) for i in (1, 2, 3)]
    rows_of_peers = [(lax.rem(my_y + dy, 8), lows) for dy in (4, 3, 5, 2, 6, 1, 7)] + [(my_y, lows[1:])]
    z_peers = [lax.rem(my_z + d, 4) for d in (2, 1, 3)]
    x_peers = [lax.rem(my_x + d, 4) for d in (2, 1, 3)]

    def hello(semaphore, where):
        pl.semaphore_signal(semaphore, inc=1, device_id=where, device_id_type=MESH)

    def wait_for(semaphore, count):
        @pl.when(count > 0)
        def _():
            pl.semaphore_wait(semaphore, count)

    def turn_of(y, place):
        usual = 4 * jnp.where(y <= 4, jnp.maximum(2 * y - 1, 0), 16 - 2 * y) + place
        return jnp.where(jnp.logical_and(band == 0, usual == 0), FFT, usual)

    my_turn = turn_of(my_y, my_low)
    earlier = jnp.where(band == 0, my_turn - 1, my_turn)
    z_shift = jnp.where(jnp.logical_and(me == 0, my_x == 0), 1, 0)
    x_shift = jnp.where(jnp.logical_and(me == 0, my_z == 0), 1, 0)

    def z_turn(z):
        return jnp.where(z < z_shift, 2, jnp.where(z < 3, z - z_shift, 3))

    def x_turn(x):
        return jnp.where(x < x_shift, 3, x - x_shift)

    my_z_turn, my_x_turn = z_turn(my_z), x_turn(my_x)

    def greet(semaphore, later):
        for y, places in rows_of_peers:
            for place in places:
                turn = turn_of(y, place)

                @pl.when(turn > my_turn if later else turn < my_turn)
                def _():
                    hello(semaphore, {"fft": y * 4 + place})

    barrier = pltpu.get_barrier_semaphore()
    greet(barrier, True)
    for z in z_peers:

        @pl.when(z_turn(z) > my_z_turn)
        def _():
            hello(barrier, {"band": my_x * 4 + z})

    for x in x_peers:

        @pl.when(x_turn(x) > my_x_turn)
        def _():
            hello(barrier, {"band": x * 4 + my_z})

    def wave_copies(b):
        return [
            pltpu.make_async_copy(
                wave.at[:, b, :, pl.ds(h * (N - HALF), HALF), :],
                wbuf.at[:, b, :, pl.ds(h * HALF, HALF), :],
                wsem.at[b, h],
            )
            for h in range(2)
        ]

    previous_copies = [
        pltpu.make_async_copy(
            previous.at[:, :, :, pl.ds(h * (N - HALF), HALF), :],
            pbuf.at[:, :, :, pl.ds(h * HALF, HALF), :],
            psem.at[h],
        )
        for h in range(2)
    ]
    small_refs = ((extent_hbm, extent), (metric_hbm, metric))
    load_v = pltpu.make_async_copy(potential, vown, lsem.at[0])
    small_copies = [pltpu.make_async_copy(a, b, lsem.at[i + 1]) for i, (a, b) in enumerate(small_refs)]
    table_refs = ((iz_hbm, iz), (iy_hbm, iy), (ix_hbm, ix), (fx_hbm, fx), (fy_hbm, fy), (fz_hbm, fz))
    table_copies = [pltpu.make_async_copy(a, b, tsem.at[i]) for i, (a, b) in enumerate(table_refs)]

    for copy in small_copies:
        copy.start()

    @pl.when(active)
    def _():
        for b in range(BANDS):
            for copy in wave_copies(b):
                copy.start()

    load_v.start()
    for copy in table_copies:
        copy.start()

    @pl.when(active)
    def _():
        for copy in previous_copies:
            copy.start()

    row = lax.broadcasted_iota(jnp.int32, (KEPT, N), 0)
    lane = lax.broadcasted_iota(jnp.int32, (KEPT, N), 1)
    natural = jnp.logical_or(lane < HALF, lane >= N - HALF)
    signed_gz = jnp.where(row < HALF, row, row - KEPT)
    place_gy = jnp.where(natural, lane, jnp.where(lane < KEPT, lane + KEPT, lane - KEPT))
    signed_gy = jnp.where(place_gy < N // 2, place_gy, place_gy - N)
    turn_sign = jnp.where(natural, -1.0, 1.0).astype(jnp.float32)

    def is_active(y):
        return jnp.logical_or(y < 2, y >= 6)

    def partner(y):
        return lax.rem(jnp.where(jnp.logical_or(y < 2, jnp.logical_or(y == 4, y == 5)), y + 2, y + 6), 8)

    def plane_of(y, place, c):
        if c < 4:
            return 4 * (y * 4 + place) + c
        return 4 * (partner(y) * 4 + place) + 3

    def keep_of(j):
        return (jnp.abs(signed_gz) <= extent[pl.ds(j, 1), :]).astype(jnp.float32)

    def both_parts(keep, real, imag):
        return keep * real + pltpu.roll(keep * imag, KEPT, axis=1)

    def to_planes():
        for b in range(BANDS):
            for copy in wave_copies(b):
                copy.wait()
        for j in range(4):
            keep = keep_of(j)
            for b in range(BANDS):
                packed = both_parts(keep, wbuf[0, b, j], wbuf[1, b, j])
                turned = pltpu.roll(packed, KEPT, axis=1) * turn_sign
                for t, part in enumerate((packed, turned)):
                    high, low = halves(part)
                    zboth[j, t * KEPT : (t + 1) * KEPT, b * N : (b + 1) * N] = high
                    zboth[j, N + t * KEPT : N + (t + 1) * KEPT, b * N : (b + 1) * N] = low
            both = dot(iz[...], zboth[j])
            both = both[:N] + both[N:]
            for b in range(BANDS):
                sbuf[pl.ds(2 * j + b, N, stride=8), :] = both[:, b * N : (b + 1) * N]
        for c in range(PLANES):
            mine = sbuf[pl.ds(pl.multiple_of(plane_of(my_y, my_low, c) * 8, 8), 8), :]
            rbuf[c, pl.ds(pl.multiple_of(slot * 8, 8), 8), :] = mine

    def scale():
        return jnp.full((1, N), 2.0, jnp.float32) / jnp.full((1, N), halfwidth[0], jnp.float32)

    def the_rest():
        for copy in previous_copies:
            copy.wait()
        step_z = (2.0 * math.pi / N) * signed_gz.astype(jnp.float32)
        step_y = (2.0 * math.pi / N) * signed_gy.astype(jnp.float32)
        plane_kinetic = metric[2] * (step_z * step_z) + metric[1] * (step_y * step_y)
        factor = scale()
        for j in range(4):
            gx = me * 4 + j
            signed_gx = jnp.where(gx < N // 2, gx, gx - N).astype(jnp.float32)
            step_x = (2.0 * math.pi / N) * signed_gx
            weight = factor * (0.5 * (metric[0] * (step_x * step_x) + plane_kinetic) - center[0])
            keep = keep_of(j)
            for b in range(BANDS):
                coefficient = both_parts(keep, wbuf[0, b, j], wbuf[1, b, j])
                base[b, j] = weight * coefficient - both_parts(keep, pbuf[0, b, j], pbuf[1, b, j])

    def send_planes(c):
        def send(y, places):
            for place in places:
                pltpu.make_async_remote_copy(
                    src_ref=sbuf.at[pl.ds(pl.multiple_of(plane_of(y, place, c) * 8, 8), 8), :],
                    dst_ref=rbuf.at[c, pl.ds(pl.multiple_of(slot * 8, 8), 8), :],
                    send_sem=fsend.at[c],
                    recv_sem=frecv.at[c],
                    device_id={"fft": y * 4 + place},
                    device_id_type=MESH,
                ).start()

        for y, places in rows_of_peers:
            if c < FEW:
                send(y, places)
            else:

                @pl.when(is_active(y))
                def _():
                    send(y, places)

    def send_columns(c):
        plane = plane_of(my_y, my_low, c)
        for y, places in rows_of_peers:

            @pl.when(is_active(y))
            def _():
                first = jnp.where(y < 2, y, y - 4) * 4
                for place in places:
                    pltpu.make_async_remote_copy(
                        src_ref=gbuf.at[c, pl.ds(pl.multiple_of((first + place) * 8, 8), 8), :],
                        dst_ref=hbuf.at[pl.ds(pl.multiple_of(plane * 8, 8), 8), :],
                        send_sem=gsend.at[c],
                        recv_sem=grecv.at[c],
                        device_id={"fft": y * 4 + place},
                        device_id_type=MESH,
                    ).start()

    def awaited(ref, send, recv):
        return pltpu.make_async_remote_copy(
            src_ref=ref, dst_ref=ref, send_sem=send, recv_sem=recv, device_id={"fft": me}, device_id_type=MESH
        )

    def send_v(where, phase, peer):
        pltpu.make_async_remote_copy(
            src_ref=where,
            dst_ref=where,
            send_sem=vsend.at[phase],
            recv_sem=vrecv.at[phase],
            device_id={"band": peer},
            device_id_type=MESH,
        ).start()

    my_rows = pl.ds(pl.multiple_of(band * 8, 8), 8)

    def send_v_along_z(z):
        @pl.when(active)
        def _():
            send_v(vbuf.at[pl.ds(0, 4), my_rows, :], PLANES, my_x * 4 + z)

        @pl.when(jnp.logical_not(active))
        def _():
            send_v(vbuf.at[pl.ds(0, FEW), my_rows, :], PLANES, my_x * 4 + z)

    def v_along_z(planes):
        return awaited(vbuf.at[pl.ds(0, planes), pl.ds(0, 24), :], vsend.at[PLANES], vrecv.at[PLANES])

    v_last_along_z = awaited(vbuf.at[4, pl.ds(0, 24), :], vsend.at[PLANES + 1], vrecv.at[PLANES + 1])

    def send_v_along_x(c):
        for x in x_peers:
            send_v(vbuf.at[c, pl.ds(pl.multiple_of(my_x * 32, 32), 32), :], c, x * 4 + my_z)

    def v_along_x(c):
        return awaited(vbuf.at[c, pl.ds(0, 96), :], vsend.at[c], vrecv.at[c])

    v_handed = pltpu.make_async_remote_copy(
        src_ref=vbuf.at[3, my_rows, :],
        dst_ref=vbuf.at[4, my_rows, :],
        send_sem=esend,
        recv_sem=erecv,
        device_id={"fft": partner(my_y) * 4 + my_low},
        device_id_type=MESH,
    )

    def work(c):
        high, low = halves(rbuf[c])
        plane = dot(jnp.concatenate([high, low, high], axis=1), iy[...])
        yre[...] = plane[:, :N]
        yim[...] = plane[:, N:]
        with jax.named_scope(f"wait_v{c}"):
            v_along_x(c).wait_recv()
        local_v = vbuf[c]
        for b in range(BANDS):
            rh, rl = halves(yre[pl.ds(b, KEPT, stride=2), :])
            ih, il = halves(yim[pl.ds(b, KEPT, stride=2), :])
            right = jnp.concatenate(
                [
                    jnp.concatenate([rh, ih], axis=1),
                    jnp.concatenate([-ih, rh], axis=1),
                    jnp.concatenate([rl, il], axis=1),
                    jnp.concatenate([-il, rl], axis=1),
                ],
                axis=0,
            )
            field = dot(ix[...], right)
            field = field[:N] + field[N:]
            rh, rl = halves(field[:, :N] * local_v)
            ih, il = halves(field[:, N:] * local_v)
            right = jnp.concatenate(
                [jnp.concatenate([rh, ih], axis=1), jnp.concatenate([rl, il], axis=1)], axis=0
            )
            both = dot(fx[...], right)
            both = both[:N] + both[N:]
            cos_part, sin_part = both[:KEPT], both[KEPT:]
            rows = slice(b * KEPT, (b + 1) * KEPT)
            high, low = halves(cos_part[:, :N] + sin_part[:, N:])
            qhigh[rows, :N] = high
            qlow[rows, :N] = low
            high, low = halves(cos_part[:, N:] - sin_part[:, :N])
            qhigh[rows, N:] = high
            qlow[rows, N:] = low
        wide = dot(qhigh[...], fy[...])
        packed = wide[:, :N] + wide[:, N:] + dot(qlow[...], fy[:, :N])
        for b in range(BANDS):
            gbuf[c, pl.ds(b, KEPT, stride=2), :] = packed[b * KEPT : (b + 1) * KEPT]
        with jax.named_scope(f"send_columns{c}"):
            send_columns(c)

        def keep_mine():
            mine = gbuf[c, pl.ds(pl.multiple_of(slot * 8, 8), 8), :]
            hbuf[pl.ds(pl.multiple_of(plane_of(my_y, my_low, c) * 8, 8), 8), :] = mine

        if c < FEW:
            pl.when(active)(keep_mine)
        else:
            keep_mine()

    with jax.named_scope("barrier"):
        wait_for(barrier, earlier + my_z_turn + my_x_turn)
        greet(ready.at[2], False)
        load_v.wait()
        for c in range(4):
            vbuf[c, my_rows, :] = vown[pl.ds(c, 8, stride=4), :]

    waits_for_first = jnp.logical_and(band == 0, me == 8)

    @pl.when(jnp.logical_not(jnp.logical_or(active, waits_for_first)))
    def _():
        v_handed.start()


    for z in z_peers:

        @pl.when(z_turn(z) < my_z_turn)
        def _():
            hello(ready.at[0], {"band": my_x * 4 + z})
            send_v_along_z(z)

    for x in x_peers:

        @pl.when(x_turn(x) < my_x_turn)
        def _():
            hello(ready.at[1], {"band": x * 4 + my_z})

    for copy in small_copies:
        copy.wait()
    table_copies[0].wait()

    @pl.when(active)
    def _():
        with jax.named_scope("planes"):
            to_planes()

    with jax.named_scope("wait_group"):
        wait_for(ready.at[2], FFT - 1 - earlier)

    @pl.when(waits_for_first)
    def _():
        v_handed.start()

    @pl.when(active)
    def _():
        with jax.named_scope("send"):
            for c in range(PLANES):
                send_planes(c)

    with jax.named_scope("wait_z"):
        wait_for(ready.at[0], 3 - my_z_turn)
    for z in z_peers:

        @pl.when(z_turn(z) > my_z_turn)
        def _():
            send_v_along_z(z)

    @pl.when(active)
    def _():
        with jax.named_scope("the_rest"):
            the_rest()

    with jax.named_scope("wait_vz"):

        @pl.when(active)
        def _():
            v_handed.wait_recv()
            for z in z_peers:
                send_v(vbuf.at[4, my_rows, :], PLANES + 1, my_x * 4 + z)
            v_along_z(4).wait_recv()

        @pl.when(jnp.logical_not(active))
        def _():
            v_along_z(FEW).wait_recv()

        wait_for(ready.at[1], 3 - my_x_turn)

    for c in range(FEW):
        send_v_along_x(c)

    @pl.when(active)
    def _():
        send_v_along_x(3)
        with jax.named_scope("wait_vlast"):
            v_last_along_z.wait_recv()
        send_v_along_x(4)

    for copy in table_copies[1:]:
        copy.wait()

    for c in range(FEW):
        with jax.named_scope(f"wait_planes{c}"):

            @pl.when(active)
            def _():
                awaited(rbuf.at[c, pl.ds(0, 8 * (ACTIVE - 1)), :], fsend.at[c], frecv.at[c]).wait_recv()

            @pl.when(jnp.logical_not(active))
            def _():
                awaited(rbuf.at[c], fsend.at[c], frecv.at[c]).wait_recv()

        work(c)

    def peers_with(c):
        return FFT - 1 if c < FEW else ACTIVE - 1

    @pl.when(active)
    def _():
        for c in range(FEW, PLANES):
            with jax.named_scope(f"wait_planes{c}"):
                awaited(rbuf.at[c, pl.ds(0, 8 * (ACTIVE - 1)), :], fsend.at[c], frecv.at[c]).wait_recv()
            work(c)
        factor = scale()
        for c in range(PLANES):
            with jax.named_scope(f"wait_columns{c}"):
                awaited(hbuf.at[pl.ds(0, 8 * peers_with(c)), :], gsend.at[c], grecv.at[c]).wait_recv()
        for j in range(4):
            h0, l0 = halves(hbuf[pl.ds(2 * j, N, stride=8), :])
            h1, l1 = halves(hbuf[pl.ds(2 * j + 1, N, stride=8), :])
            right = jnp.concatenate(
                [jnp.concatenate([h0, h1], axis=1), jnp.concatenate([l0, l1], axis=1)], axis=0
            )
            both = dot(fz[...], right)
            both = both[:N] + both[N:]
            keep = keep_of(j)
            keep = keep + pltpu.roll(keep, KEPT, axis=1)
            for b in range(BANDS):
                cos_part = both[:KEPT, b * N : (b + 1) * N]
                sin_part = both[KEPT:, b * N : (b + 1) * N]
                applied = cos_part - turn_sign * pltpu.roll(sin_part, KEPT, axis=1)
                out[b, j] = keep * (factor * applied) + base[b, j]

    with jax.named_scope("wait_sends"):

        @pl.when(active)
        def _():
            v_along_z(4).wait_send()
            v_last_along_z.wait_send()
            for c in range(FEW, PLANES):
                v_along_x(c).wait_send()
            for c in range(PLANES):
                awaited(sbuf.at[pl.ds(0, 8 * peers_with(c)), :], fsend.at[c], frecv.at[c]).wait_send()
                awaited(gbuf.at[c, pl.ds(0, 8 * (ACTIVE - 1)), :], gsend.at[c], grecv.at[c]).wait_send()

        @pl.when(jnp.logical_not(active))
        def _():
            v_handed.wait_send()
            v_along_z(FEW).wait_send()
            for c in range(FEW):
                awaited(gbuf.at[c], gsend.at[c], grecv.at[c]).wait_send()

        for c in range(FEW):
            v_along_x(c).wait_send()


def expand(packed, out, obuf, sem):
    me = lax.axis_index("fft")
    active = jnp.logical_or(me < ACTIVE // 2, me >= FFT - ACTIVE // 2)
    lane = lax.broadcasted_iota(jnp.int32, (KEPT, N), 1)
    natural = jnp.logical_or(lane < HALF, lane >= N - HALF)
    copies = [pltpu.make_async_copy(obuf.at[:, b], out.at[:, b], sem.at[b]) for b in range(BANDS)]

    @pl.when(active)
    def _():
        for b in range(BANDS):
            for j in range(4):
                both = packed[b, j]
                for t, part in enumerate((both, pltpu.roll(both, KEPT, axis=1))):
                    part = jnp.where(natural, part, 0.0)
                    obuf[t, b, j, :HALF, :] = part[:HALF]
                    obuf[t, b, j, HALF : N - HALF, :] = jnp.zeros((KEPT, N), jnp.float32)
                    obuf[t, b, j, N - HALF :, :] = part[HALF:]
            copies[b].start()

    @pl.when(jnp.logical_not(active))
    def _():
        obuf[...] = jnp.zeros_like(obuf)
        for copy in copies:
            copy.start()

    for copy in copies:
        copy.wait()


def local(tables, wave, previous, potential, column_extent, metric, center, halfwidth):
    any_spec = pl.BlockSpec(memory_space=pltpu.HBM)
    vmem_spec = pl.BlockSpec(memory_space=pltpu.VMEM)
    smem_spec = pl.BlockSpec(memory_space=pltpu.SMEM)
    f32, bf16 = jnp.float32, jnp.bfloat16
    dma = pltpu.SemaphoreType.DMA
    packed = pl.pallas_call(
        kernel,
        out_shape=pltpu.VMEM((BANDS, 4, KEPT, N), f32),
        in_specs=[any_spec] * 5 + [smem_spec] * 2 + [any_spec] * 6,
        out_specs=vmem_spec,
        scratch_shapes=[
            pltpu.VMEM((4, N), jnp.int32),
            pltpu.SMEM((3,), f32),
            pltpu.VMEM((2, BANDS, 4, KEPT, N), f32),
            pltpu.VMEM((2, BANDS, 4, KEPT, N), f32),
            pltpu.VMEM((PLANES, N, N), f32),
            *[pltpu.VMEM(table.shape, bf16) for table in tables],
            pltpu.VMEM((32, N), f32),
            pltpu.VMEM((4, 2 * N, 2 * N), bf16),
            pltpu.VMEM((8 * N, N), f32),
            pltpu.VMEM((PLANES, N, N), f32),
            pltpu.VMEM((N, N), f32),
            pltpu.VMEM((N, N), f32),
            pltpu.VMEM((N, 2 * N), bf16),
            pltpu.VMEM((N, 2 * N), bf16),
            pltpu.VMEM((PLANES, N, N), f32),
            pltpu.VMEM((8 * N, N), f32),
            pltpu.VMEM((BANDS, 4, KEPT, N), f32),
            dma((BANDS, 2)),
            dma((2,)),
            dma((6,)),
            dma((3,)),
            dma((PLANES,)),
            dma((PLANES,)),
            dma((PLANES,)),
            dma((PLANES,)),
            dma((PLANES + 2,)),
            dma((PLANES + 2,)),
            dma,
            dma,
            pltpu.SemaphoreType.REGULAR((3,)),
        ],
        compiler_params=pltpu.CompilerParams(
            collective_id=0, has_side_effects=True, vmem_limit_bytes=24 * 1024 * 1024
        ),
    )(
        *[
            pltpu.with_memory_space_constraint(value, pltpu.HBM)
            for value in (wave, previous, potential.reshape(32, N), column_extent, metric)
        ],
        center,
        halfwidth,
        *[pltpu.with_memory_space_constraint(table, pltpu.HBM) for table in tables],
    )
    return pl.pallas_call(
        expand,
        out_shape=jax.ShapeDtypeStruct(wave.shape, f32),
        in_specs=[vmem_spec],
        out_specs=any_spec,
        scratch_shapes=[pltpu.VMEM((2, BANDS, 4, N, N), f32), dma((BANDS,))],
        compiler_params=pltpu.CompilerParams(vmem_limit_bytes=8 * 1024 * 1024),
    )(packed)


def solution(mesh):
    tables = [jnp.asarray(table) for table in make_tables()]
    in_specs = (
        P(None, "band", "fft", None, None),
        P(None, "band", "fft", None, None),
        P("band", "fft", None),
        P("fft", None),
        P(),
        P(),
        P(),
    )
    out_specs = P(None, "band", "fft", None, None)
    return jax.shard_map(
        functools.partial(local, tables), mesh=mesh, in_specs=in_specs, out_specs=out_specs, check_vma=False
    )
```

time: 44.8 us -> 38.9 us (0.87)
  Pallas kernels: 41 us -> 37.5 us
  local copies, waits for them, and re-layouts: 2.3 us -> 0 us
    pallas_call x1 -> x2, Pallas kernels: 41 us -> 37.5 us  [the longest x1 36.4 us: local(): pl.pallas_call(kernel, out_shape=pltpu.VMEM((BANDS, 4, KEPT, N), f32), in...]
    unnamed x1 -> x0, local copies, waits for them, and re-layouts: 2.3 us -> none
where the time goes in v2:
time: 38.9 us; the launch traced here: 38.8 us
  Pallas kernels  37.5 us (96%)
  between operations  1.3 us (3%)
    pallas_call x1, Pallas kernels, local(): pl.pallas_call(kernel, out_shape=pltpu.VMEM((BANDS, 4, KEPT, N), f32), in...  36.4 us
    pallas_call x1, Pallas kernels, local(): pl.pallas_call(expand, out_shape=jax.ShapeDtypeStruct(wave.shape, f32), i...  1.09 us

profile of v2, /device:TPU:1, one launch (start us, length us, event | category | flops | bytes accessed | tf_op | source)
XLA Modules:
  0.0 38.8 jit_solution(17177699306605874629)
XLA Ops:
  1.3 36.4 %shard_map.127.packed = f32[2,4,64,128]{3,2,1,0:T(8,128)S(1)} custom-call(f32[2,2,4,128,128]{4,3,2,1,0:T(8,128)} %wave.1, f32[2,2,4,128,128]{4,3,2,1,0:T(8,128)} %previous.1, f32[32,128]{1,0:T(8,128)} %bitcast.1, s32[4,128]{1,0:T(4,128)} %extent_hbm.1, f32[3]{0:T(128)} %metric_hbm.1, f32[1]{0:T(128)S(6)} %copy.14.center, f32[1]{0:T(128)S(6)} %copy.15.halfwidth, ...), custom_call_target="tpu_custom_call" | custom-call | tf_op jit(solution)/shard_map/pallas_call | solution.py:655
  37.7 1.1 %shard_map.128 = f32[2,2,4,128,128]{4,3,2,1,0:T(8,128)} custom-call(f32[2,4,64,128]{3,2,1,0:T(8,128)S(1)} %shard_map.127.packed), custom_call_target="tpu_custom_call" | custom-call | tf_op jit(solution)/shard_map/pallas_call | solution.py:704

commit v3 on v2

--- a/solution.py
+++ b/solution.py
@@ -138,6 +138,7 @@
     rbuf,
     yre,
     yim,
+    fbuf,
     qhigh,
     qlow,
     gbuf,
@@ -177,7 +178,7 @@
             pl.semaphore_wait(semaphore, count)
 
     def turn_of(y, place):
-        usual = 4 * jnp.where(y <= 4, jnp.maximum(2 * y - 1, 0), 16 - 2 * y) + place
+        usual = 4 * jnp.where(y < 4, y, 11 - y) + place
         return jnp.where(jnp.logical_and(band == 0, usual == 0), FFT, usual)
 
     my_turn = turn_of(my_y, my_low)
@@ -186,24 +187,87 @@
     x_shift = jnp.where(jnp.logical_and(me == 0, my_z == 0), 1, 0)
 
     def z_turn(z):
-        return jnp.where(z < z_shift, 2, jnp.where(z < 3, z - z_shift, 3))
+        return jnp.where(z < z_shift, 1, jnp.where(z == 1, 1 - z_shift, z))
 
     def x_turn(x):
         return jnp.where(x < x_shift, 3, x - x_shift)
 
     my_z_turn, my_x_turn = z_turn(my_z), x_turn(my_x)
 
+    late = jnp.logical_and(band == 0, me == 0)
+    side_2 = jnp.logical_and(my_y >= 2, my_y < 4)
+    side_6 = my_y >= 6
+
+    my_row = jnp.where(my_y < 4, my_y, 11 - my_y)
+    y_order = (4, 5, 6, 3, 7, 2, 1, 0)
+
     def greet(semaphore, later):
-        for y, places in rows_of_peers:
-            for place in places:
-                turn = turn_of(y, place)
-
-                @pl.when(turn > my_turn if later else turn < my_turn)
+        def to(y, line, core):
+            place = 2 * line + core
+            if y == 0 and core == 0 and not later:
+
+                @pl.when(jnp.logical_or(band != 0, line != 0))
                 def _():
                     hello(semaphore, {"fft": y * 4 + place})
-
+            else:
+                hello(semaphore, {"fft": y * 4 + place})
+
+        for y in y_order:
+            y_row = y if y < 4 else 11 - y
+            near = y_row > my_row if later else y_row < my_row
+            if later and y >= 6:
+                near = near & jnp.logical_not(side_2)
+            if not later and 2 <= y < 4:
+                near = near & jnp.logical_not(side_6)
+
+            @pl.when(near)
+            def _():
+                for line in range(2):
+                    for core in range(2):
+                        to(y, line, core)
+
+        for place in range(4):
+
+            @pl.when(place > my_low if later else place < my_low)
+            def _():
+                if place > 0:
+                    hello(semaphore, {"fft": my_y * 4 + place})
+                else:
+
+                    @pl.when(jnp.logical_or(band != 0, my_y > 0))
+                    def _():
+                        hello(semaphore, {"fft": my_y * 4})
+
+    def greet_all(semaphore):
+        for y in range(FFT // 4):
+            for place in range(4):
+                if y + place > 0:
+                    hello(semaphore, {"fft": y * 4 + place})
+
+    def is_late_row(y):
+        return jnp.logical_and(band == 0, y == 0)
+
+    load_v = pltpu.make_async_copy(potential, vown, lsem.at[0])
+    load_v.start()
     barrier = pltpu.get_barrier_semaphore()
-    greet(barrier, True)
+    direct = jnp.logical_not(active)
+    early = jnp.logical_and(direct, my_z < 2)
+    tardy = jnp.logical_and(direct, my_z >= 2)
+
+    @pl.when(jnp.logical_not(late))
+    def _():
+        greet(barrier, True)
+
+    @pl.when(jnp.logical_and(band == 0, me > 0))
+    def _():
+        hello(barrier, {"fft": 0})
+
+    @pl.when(my_z < 2)
+    def _():
+        for z in (2, 3):
+            for x in x_peers:
+                hello(barrier, {"band": x * 4 + z})
+
     for z in z_peers:
 
         @pl.when(z_turn(z) > my_z_turn)
@@ -235,7 +299,6 @@
         for h in range(2)
     ]
     small_refs = ((extent_hbm, extent), (metric_hbm, metric))
-    load_v = pltpu.make_async_copy(potential, vown, lsem.at[0])
     small_copies = [pltpu.make_async_copy(a, b, lsem.at[i + 1]) for i, (a, b) in enumerate(small_refs)]
     table_refs = ((iz_hbm, iz), (iy_hbm, iy), (ix_hbm, ix), (fx_hbm, fx), (fy_hbm, fy), (fz_hbm, fz))
     table_copies = [pltpu.make_async_copy(a, b, tsem.at[i]) for i, (a, b) in enumerate(table_refs)]
@@ -249,7 +312,6 @@
             for copy in wave_copies(b):
                 copy.start()
 
-    load_v.start()
     for copy in table_copies:
         copy.start()
 
@@ -275,6 +337,8 @@
     def plane_of(y, place, c):
         if c < 4:
             return 4 * (y * 4 + place) + c
+        if isinstance(y, int):
+            return 4 * ((y + 2 if y < 2 else y - 2) * 4 + place) + 3
         return 4 * (partner(y) * 4 + place) + 3
 
     def keep_of(j):
@@ -324,43 +388,80 @@
                 coefficient = both_parts(keep, wbuf[0, b, j], wbuf[1, b, j])
                 base[b, j] = weight * coefficient - both_parts(keep, pbuf[0, b, j], pbuf[1, b, j])
 
-    def send_planes(c):
-        def send(y, places):
-            for place in places:
-                pltpu.make_async_remote_copy(
-                    src_ref=sbuf.at[pl.ds(pl.multiple_of(plane_of(y, place, c) * 8, 8), 8), :],
-                    dst_ref=rbuf.at[c, pl.ds(pl.multiple_of(slot * 8, 8), 8), :],
-                    send_sem=fsend.at[c],
-                    recv_sem=frecv.at[c],
-                    device_id={"fft": y * 4 + place},
-                    device_id_type=MESH,
-                ).start()
-
-        for y, places in rows_of_peers:
-            if c < FEW:
-                send(y, places)
+    def send_plane(c, y, place):
+        pltpu.make_async_remote_copy(
+            src_ref=sbuf.at[pl.ds(pl.multiple_of(plane_of(y, place, c) * 8, 8), 8), :],
+            dst_ref=rbuf.at[c, pl.ds(pl.multiple_of(slot * 8, 8), 8), :],
+            send_sem=fsend.at[c],
+            recv_sem=frecv.at[c],
+            device_id={"fft": y * 4 + place},
+            device_id_type=MESH,
+        ).start()
+
+    def to_others(y, send):
+        @pl.when(my_y == y)
+        def _():
+            for place in lows[1:]:
+                send(y, place)
+
+        @pl.when(my_y != y)
+        def _():
+            for place in lows:
+                send(y, place)
+
+    def send_planes(c, order):
+        def send(y, place):
+            send_plane(c, y, place)
+
+        def unless_late(y, place):
+            @pl.when(jnp.logical_and(place > 0, y * 4 + place != me))
+            def _():
+                send(y, place)
+
+        for y in order:
+            if 2 <= y < 6:
+                if c < FEW:
+                    for place in lows:
+                        send(y, place)
+            elif y > 0:
+                to_others(y, send)
             else:
 
-                @pl.when(is_active(y))
+                @pl.when(band == 0)
                 def _():
-                    send(y, places)
+                    for place in lows:
+                        unless_late(0, place)
+
+                @pl.when(band != 0)
+                def _():
+                    to_others(0, send)
 
     def send_columns(c):
         plane = plane_of(my_y, my_low, c)
-        for y, places in rows_of_peers:
-
-            @pl.when(is_active(y))
-            def _():
-                first = jnp.where(y < 2, y, y - 4) * 4
-                for place in places:
-                    pltpu.make_async_remote_copy(
-                        src_ref=gbuf.at[c, pl.ds(pl.multiple_of((first + place) * 8, 8), 8), :],
-                        dst_ref=hbuf.at[pl.ds(pl.multiple_of(plane * 8, 8), 8), :],
-                        send_sem=gsend.at[c],
-                        recv_sem=grecv.at[c],
-                        device_id={"fft": y * 4 + place},
-                        device_id_type=MESH,
-                    ).start()
+
+        def send(y, place):
+            first = (y if y < 2 else y - 4) * 4
+            pltpu.make_async_remote_copy(
+                src_ref=gbuf.at[c, pl.ds(pl.multiple_of((first + place) * 8, 8), 8), :],
+                dst_ref=hbuf.at[pl.ds(pl.multiple_of(plane * 8, 8), 8), :],
+                send_sem=gsend.at[c],
+                recv_sem=grecv.at[c],
+                device_id={"fft": y * 4 + place},
+                device_id_type=MESH,
+            ).start()
+
+        @pl.when(active)
+        def _():
+            for y in (7, 0, 6, 1):
+                to_others(y, send)
+
+        if c < FEW:
+
+            @pl.when(jnp.logical_not(active))
+            def _():
+                for y in (7, 0, 6, 1):
+                    for place in lows:
+                        send(y, place)
 
     def awaited(ref, send, recv):
         return pltpu.make_async_remote_copy(
@@ -379,26 +480,41 @@
 
     my_rows = pl.ds(pl.multiple_of(band * 8, 8), 8)
 
-    def send_v_along_z(z):
-        @pl.when(active)
-        def _():
-            send_v(vbuf.at[pl.ds(0, 4), my_rows, :], PLANES, my_x * 4 + z)
-
-        @pl.when(jnp.logical_not(active))
-        def _():
-            send_v(vbuf.at[pl.ds(0, FEW), my_rows, :], PLANES, my_x * 4 + z)
-
-    def v_along_z(planes):
-        return awaited(vbuf.at[pl.ds(0, planes), pl.ds(0, 24), :], vsend.at[PLANES], vrecv.at[PLANES])
-
-    v_last_along_z = awaited(vbuf.at[4, pl.ds(0, 24), :], vsend.at[PLANES + 1], vrecv.at[PLANES + 1])
-
-    def send_v_along_x(c):
+    def v_part(planes, rows):
+        return vbuf.at[pl.ds(0, planes), rows, :]
+
+    def v_rows(z):
+        return pl.ds(pl.multiple_of(my_x * 32 + z * 8, 8), 8)
+
+    def for_kind(function):
+        pl.when(active)(lambda: function(4))
+        pl.when(jnp.logical_not(active))(lambda: function(FEW))
+
+    def takes_z(z):
+        return jnp.logical_not(jnp.logical_and(tardy, z < 2))
+
+    def send_v_along_z(z, turn):
+        @pl.when(takes_z(z))
+        def _():
+            for_kind(lambda planes: send_v(v_part(planes, my_rows), turn, my_x * 4 + z))
+
+    def v_along_z(planes, turn):
+        return awaited(v_part(planes, pl.ds(0, 8)), vsend.at[turn], vrecv.at[turn])
+
+    def send_v_along_x(z):
         for x in x_peers:
-            send_v(vbuf.at[c, pl.ds(pl.multiple_of(my_x * 32, 32), 32), :], c, x * 4 + my_z)
-
-    def v_along_x(c):
-        return awaited(vbuf.at[c, pl.ds(0, 96), :], vsend.at[c], vrecv.at[c])
+            for_kind(lambda planes: send_v(v_part(planes, v_rows(z)), 4, x * 4 + my_z))
+
+    def send_v_directly(part, phase):
+        for z in range(2):
+            for x in x_peers + [my_x]:
+                send_v(part, phase, x * 4 + z)
+
+    def v_wait(planes, phase, rows):
+        return awaited(v_part(planes, pl.ds(0, rows)), vsend.at[phase], vrecv.at[phase])
+
+    def v_last(phase, rows):
+        return awaited(vbuf.at[4, pl.ds(0, rows), :], vsend.at[phase], vrecv.at[phase])
 
     v_handed = pltpu.make_async_remote_copy(
         src_ref=vbuf.at[3, my_rows, :],
@@ -409,14 +525,23 @@
         device_id_type=MESH,
     )
 
-    def work(c):
+    def field(c):
+        with jax.named_scope(f"wait_planes{c}"):
+
+            @pl.when(active)
+            def _():
+                awaited(rbuf.at[c, pl.ds(0, 8 * (ACTIVE - 1)), :], fsend.at[c], frecv.at[c]).wait_recv()
+
+            if c < FEW:
+
+                @pl.when(jnp.logical_not(active))
+                def _():
+                    awaited(rbuf.at[c], fsend.at[c], frecv.at[c]).wait_recv()
+
         high, low = halves(rbuf[c])
         plane = dot(jnp.concatenate([high, low, high], axis=1), iy[...])
         yre[...] = plane[:, :N]
         yim[...] = plane[:, N:]
-        with jax.named_scope(f"wait_v{c}"):
-            v_along_x(c).wait_recv()
-        local_v = vbuf[c]
         for b in range(BANDS):
             rh, rl = halves(yre[pl.ds(b, KEPT, stride=2), :])
             ih, il = halves(yim[pl.ds(b, KEPT, stride=2), :])
@@ -429,10 +554,41 @@
                 ],
                 axis=0,
             )
-            field = dot(ix[...], right)
-            field = field[:N] + field[N:]
-            rh, rl = halves(field[:, :N] * local_v)
-            ih, il = halves(field[:, N:] * local_v)
+            both = dot(ix[...], right)
+            fbuf[c, b] = both[:N] + both[N:]
+
+    def back(c):
+        if c == 0:
+            with jax.named_scope("wait_v"):
+
+                def arrived(planes):
+                    @pl.when(early)
+                    def _():
+                        v_wait(planes, 4, 48).wait_recv()
+                        v_wait(planes, 7, 64).wait_recv()
+
+                    @pl.when(jnp.logical_not(early))
+                    def _():
+                        v_wait(planes, 4, 96).wait_recv()
+
+                for_kind(arrived)
+        if c == 4:
+            with jax.named_scope("wait_v4"):
+
+
+                @pl.when(my_z < 2)
+                def _():
+                    v_last(6, 48).wait_recv()
+                    v_last(8, 64).wait_recv()
+
+                @pl.when(my_z >= 2)
+                def _():
+                    v_last(6, 96).wait_recv()
+
+        local_v = vbuf[c]
+        for b in range(BANDS):
+            rh, rl = halves(fbuf[c, b, :, :N] * local_v)
+            ih, il = halves(fbuf[c, b, :, N:] * local_v)
             right = jnp.concatenate(
                 [jnp.concatenate([rh, ih], axis=1), jnp.concatenate([rl, il], axis=1)], axis=0
             )
@@ -463,12 +619,23 @@
             keep_mine()
 
     with jax.named_scope("barrier"):
-        wait_for(barrier, earlier + my_z_turn + my_x_turn)
-        greet(ready.at[2], False)
+        wait_for(barrier, earlier + my_z_turn + my_x_turn + jnp.where(my_z >= 2, 6, 0) - jnp.where(side_6, 8, 0))
         load_v.wait()
         for c in range(4):
             vbuf[c, my_rows, :] = vown[pl.ds(c, 8, stride=4), :]
 
+    @pl.when(tardy)
+    def _():
+        send_v_directly(v_part(FEW, my_rows), 7)
+
+    @pl.when(late)
+    def _():
+        greet_all(ready.at[3])
+
+    @pl.when(jnp.logical_not(late))
+    def _():
+        greet(ready.at[2], False)
+
     waits_for_first = jnp.logical_and(band == 0, me == 8)
 
     @pl.when(jnp.logical_not(jnp.logical_or(active, waits_for_first)))
@@ -481,7 +648,7 @@
         @pl.when(z_turn(z) < my_z_turn)
         def _():
             hello(ready.at[0], {"band": my_x * 4 + z})
-            send_v_along_z(z)
+            send_v_along_z(z, my_z_turn)
 
     for x in x_peers:
 
@@ -498,72 +665,131 @@
         with jax.named_scope("planes"):
             to_planes()
 
+    def hand_on(z, later):
+        @pl.when(active & (z_turn(z) > my_z_turn if later else z_turn(z) < my_z_turn) & jnp.logical_not((my_z >= 2) & (z < 2)))
+        def _():
+            send_v(vbuf.at[4, my_rows, :], 5, my_x * 4 + z)
+
+    @pl.when(jnp.logical_and(active, jnp.logical_not(late)))
+    def _():
+        with jax.named_scope("wait_handed"):
+            v_handed.wait_recv()
+        for z in z_peers:
+            hand_on(z, False)
+
+        @pl.when(my_z >= 2)
+        def _():
+            send_v_directly(vbuf.at[4, my_rows, :], 8)
+
     with jax.named_scope("wait_group"):
-        wait_for(ready.at[2], FFT - 1 - earlier)
-
-    @pl.when(waits_for_first)
-    def _():
-        v_handed.start()
-
-    @pl.when(active)
-    def _():
-        with jax.named_scope("send"):
+        wait_for(
+            ready.at[2],
+            jnp.where(late, 0, jnp.where(band == 0, FFT - 2, FFT - 1) - earlier - jnp.where(side_2, 8, 0)),
+        )
+
+
+    @pl.when(my_y == 1)
+    def _():
+        for y in (7, 6):
+            hello(ready.at[4], {"fft": y * 4 + my_low})
+
+    with jax.named_scope("send"):
+
+        @pl.when(my_y < 2)
+        def _():
             for c in range(PLANES):
-                send_planes(c)
+                send_planes(c, (4, 3, 5, 2, 6, 7, 1, 0))
+
+        @pl.when(side_6)
+        def _():
+            for c in range(2):
+                send_planes(c, (4, 5, 1, 0, 6, 7))
+            pl.semaphore_wait(ready.at[4], 1)
+            for c in range(2):
+                send_planes(c, (3, 2))
+            for c in range(2, PLANES):
+                send_planes(c, (3, 4, 2, 5, 1, 0, 6, 7))
 
     with jax.named_scope("wait_z"):
         wait_for(ready.at[0], 3 - my_z_turn)
+
+    @pl.when(jnp.logical_not(late))
+    def _():
+        for z in z_peers:
+            hand_on(z, True)
+
     for z in z_peers:
 
         @pl.when(z_turn(z) > my_z_turn)
         def _():
-            send_v_along_z(z)
+            send_v_along_z(z, my_z_turn)
+
+    with jax.named_scope("wait_x"):
+        wait_for(ready.at[1], 3 - my_x_turn)
+    send_v_along_x(my_z)
 
     @pl.when(active)
     def _():
         with jax.named_scope("the_rest"):
             the_rest()
 
-    with jax.named_scope("wait_vz"):
+    def forward_v(turn, z):
+        @pl.when(turn != my_z_turn if turn < 2 else jnp.logical_and(turn != my_z_turn, jnp.logical_not(early)))
+        def _():
+            with jax.named_scope(f"wait_vz{turn}"):
+                for_kind(lambda planes: v_along_z(planes, turn).wait_recv())
+            send_v_along_x(z)
+
+    def z_of(turn):
+        return jnp.abs(turn - z_shift) if turn < 2 else turn
+
+    for turn in range(2):
+        forward_v(turn, z_of(turn))
+
+    @pl.when(jnp.logical_and(band == 0, me > 0))
+    def _():
+        with jax.named_scope("wait_late"):
+            pl.semaphore_wait(ready.at[3], 1)
+
+        @pl.when(me == 8)
+        def _():
+            v_handed.start()
 
         @pl.when(active)
         def _():
-            v_handed.wait_recv()
-            for z in z_peers:
-                send_v(vbuf.at[4, my_rows, :], PLANES + 1, my_x * 4 + z)
-            v_along_z(4).wait_recv()
-
-        @pl.when(jnp.logical_not(active))
-        def _():
-            v_along_z(FEW).wait_recv()
-
-        wait_for(ready.at[1], 3 - my_x_turn)
-
-    for c in range(FEW):
-        send_v_along_x(c)
-
-    @pl.when(active)
-    def _():
-        send_v_along_x(3)
-        with jax.named_scope("wait_vlast"):
-            v_last_along_z.wait_recv()
-        send_v_along_x(4)
+            for c in range(PLANES):
+                send_plane(c, 0, 0)
+
+    forward_v(2, z_of(2))
+
+    forward_v(3, z_of(3))
+
+    @pl.when(late)
+    def _():
+        v_handed.wait_recv()
+        for z in z_peers:
+            hand_on(z, False)
+            hand_on(z, True)
 
     for copy in table_copies[1:]:
         copy.wait()
 
+    def forward_last():
+        with jax.named_scope("wait_vlast"):
+
+            def forward(blocks):
+                v_last(5, 8 * blocks - 8 if blocks > 2 else 8).wait_recv()
+                for x in x_peers:
+                    send_v(vbuf.at[4, pl.ds(pl.multiple_of(my_x * 32, 32), 8 * blocks), :], 6, x * 4 + my_z)
+
+            pl.when(my_z < 2)(lambda: forward(2))
+            pl.when(my_z >= 2)(lambda: forward(4))
+
     for c in range(FEW):
-        with jax.named_scope(f"wait_planes{c}"):
-
-            @pl.when(active)
-            def _():
-                awaited(rbuf.at[c, pl.ds(0, 8 * (ACTIVE - 1)), :], fsend.at[c], frecv.at[c]).wait_recv()
-
-            @pl.when(jnp.logical_not(active))
-            def _():
-                awaited(rbuf.at[c], fsend.at[c], frecv.at[c]).wait_recv()
-
-        work(c)
+        field(c)
+        back(c)
+        if c == 0:
+            pl.when(active)(forward_last)
 
     def peers_with(c):
         return FFT - 1 if c < FEW else ACTIVE - 1
@@ -571,9 +797,8 @@
     @pl.when(active)
     def _():
         for c in range(FEW, PLANES):
-            with jax.named_scope(f"wait_planes{c}"):
-                awaited(rbuf.at[c, pl.ds(0, 8 * (ACTIVE - 1)), :], fsend.at[c], frecv.at[c]).wait_recv()
-            work(c)
+            field(c)
+            back(c)
         factor = scale()
         for c in range(PLANES):
             with jax.named_scope(f"wait_columns{c}"):
@@ -598,10 +823,18 @@
 
         @pl.when(active)
         def _():
-            v_along_z(4).wait_send()
-            v_last_along_z.wait_send()
-            for c in range(FEW, PLANES):
-                v_along_x(c).wait_send()
+
+            @pl.when(my_z < 2)
+            def _():
+                v_last(5, 24).wait_send()
+                v_last(6, 48).wait_send()
+
+            @pl.when(my_z >= 2)
+            def _():
+                v_last(5, 8).wait_send()
+                v_last(6, 96).wait_send()
+                v_last(8, 64).wait_send()
+
             for c in range(PLANES):
                 awaited(sbuf.at[pl.ds(0, 8 * peers_with(c)), :], fsend.at[c], frecv.at[c]).wait_send()
                 awaited(gbuf.at[c, pl.ds(0, 8 * (ACTIVE - 1)), :], gsend.at[c], grecv.at[c]).wait_send()
@@ -609,12 +842,28 @@
         @pl.when(jnp.logical_not(active))
         def _():
             v_handed.wait_send()
-            v_along_z(FEW).wait_send()
             for c in range(FEW):
                 awaited(gbuf.at[c], gsend.at[c], grecv.at[c]).wait_send()
 
-        for c in range(FEW):
-            v_along_x(c).wait_send()
+        def v_sent(planes):
+            @pl.when(early)
+            def _():
+                v_wait(planes, 4, 48).wait_send()
+
+            @pl.when(jnp.logical_not(early))
+            def _():
+                v_wait(planes, 4, 96).wait_send()
+
+            @pl.when(tardy)
+            def _():
+                awaited(v_part(planes, pl.ds(0, 8)), vsend.at[my_z_turn], vrecv.at[4]).wait_send()
+                v_wait(planes, 7, 64).wait_send()
+
+            @pl.when(jnp.logical_not(tardy))
+            def _():
+                awaited(v_part(planes, pl.ds(0, 24)), vsend.at[my_z_turn], vrecv.at[4]).wait_send()
+
+        for_kind(v_sent)
 
 
 def expand(packed, out, obuf, sem):
@@ -670,6 +919,7 @@
             pltpu.VMEM((PLANES, N, N), f32),
             pltpu.VMEM((N, N), f32),
             pltpu.VMEM((N, N), f32),
+            pltpu.VMEM((PLANES, BANDS, N, 2 * N), f32),
             pltpu.VMEM((N, 2 * N), bf16),
             pltpu.VMEM((N, 2 * N), bf16),
             pltpu.VMEM((PLANES, N, N), f32),
@@ -683,11 +933,11 @@
             dma((PLANES,)),
             dma((PLANES,)),
             dma((PLANES,)),
-            dma((PLANES + 2,)),
-            dma((PLANES + 2,)),
+            dma((9,)),
+            dma((9,)),
             dma,
             dma,
-            pltpu.SemaphoreType.REGULAR((3,)),
+            pltpu.SemaphoreType.REGULAR((5,)),
         ],
         compiler_params=pltpu.CompilerParams(
             collective_id=0, has_side_effects=True, vmem_limit_bytes=24 * 1024 * 1024

time: 38.9 us -> 37.4 us (0.961)
  Pallas kernels: 37.5 us -> 35.9 us
    pallas_call x1, Pallas kernels: 36.4 us -> 34.8 us  [local(): pl.pallas_call(kernel, out_shape=pltpu.VMEM((BANDS, 4, KEPT, N), f32), in...]
where the time goes in v3:
time: 37.4 us; the launch traced here: 37.2 us
  Pallas kernels  35.9 us (96%)
  between operations  1.3 us (3%)
    pallas_call x1, Pallas kernels, local(): pl.pallas_call(kernel, out_shape=pltpu.VMEM((BANDS, 4, KEPT, N), f32), in...  34.8 us
    pallas_call x1, Pallas kernels, local(): pl.pallas_call(expand, out_shape=jax.ShapeDtypeStruct(wave.shape, f32), i...  1.09 us

profile of v3, /device:TPU:1, one launch (start us, length us, event | category | flops | bytes accessed | tf_op | source)
XLA Modules:
  0.0 37.2 jit_solution(2369670623820627704)
XLA Ops:
  1.3 34.8 %shard_map.127.packed = f32[2,4,64,128]{3,2,1,0:T(8,128)S(1)} custom-call(f32[2,2,4,128,128]{4,3,2,1,0:T(8,128)} %wave.1, f32[2,2,4,128,128]{4,3,2,1,0:T(8,128)} %previous.1, f32[32,128]{1,0:T(8,128)} %bitcast.1, s32[4,128]{1,0:T(4,128)} %extent_hbm.1, f32[3]{0:T(128)} %metric_hbm.1, f32[1]{0:T(128)S(6)} %copy.14.center, f32[1]{0:T(128)S(6)} %copy.15.halfwidth, ...), custom_call_target="tpu_custom_call" | custom-call | tf_op jit(solution)/shard_map/pallas_call | solution.py:904
  36.1 1.1 %shard_map.128 = f32[2,2,4,128,128]{4,3,2,1,0:T(8,128)} custom-call(f32[2,4,64,128]{3,2,1,0:T(8,128)S(1)} %shard_map.127.packed), custom_call_target="tpu_custom_call" | custom-call | tf_op jit(solution)/shard_map/pallas_call | solution.py:954

commit v4 on v3

--- a/solution.py
+++ b/solution.py
@@ -17,6 +17,7 @@
 BANDS = 2
 PLANES = 5
 FEW = 3
+FIRST = (0,)
 MESH = pl.DeviceIdType.MESH
 
 
@@ -197,12 +198,13 @@
     late = jnp.logical_and(band == 0, me == 0)
     side_2 = jnp.logical_and(my_y >= 2, my_y < 4)
     side_6 = my_y >= 6
+    later_rows = jnp.where(late, 0, jnp.where(my_y == 0, 12, jnp.where(my_y == 1, 8, jnp.where(my_y == 7, 4, 0))))
 
     my_row = jnp.where(my_y < 4, my_y, 11 - my_y)
     y_order = (4, 5, 6, 3, 7, 2, 1, 0)
 
     def greet(semaphore, later):
-        def to(y, line, core):
+        def to(y, line, core, semaphore):
             place = 2 * line + core
             if y == 0 and core == 0 and not later:
 
@@ -220,11 +222,16 @@
             if not later and 2 <= y < 4:
                 near = near & jnp.logical_not(side_6)
 
-            @pl.when(near)
-            def _():
+            def row(semaphore):
                 for line in range(2):
                     for core in range(2):
-                        to(y, line, core)
+                        to(y, line, core, semaphore)
+
+            if later or 2 <= y < 6:
+                pl.when(near)(lambda: row(semaphore))
+            else:
+                pl.when(near & active)(lambda: row(ready.at[5]))
+                pl.when(near & jnp.logical_not(active))(lambda: row(semaphore))
 
         for place in range(4):
 
@@ -409,32 +416,36 @@
             for place in lows:
                 send(y, place)
 
-    def send_planes(c, order):
+    def send_row(c, y):
+        def unless_late(place):
+            @pl.when(jnp.logical_and(place > 0, y * 4 + place != me))
+            def _():
+                send_plane(c, y, place)
+
         def send(y, place):
             send_plane(c, y, place)
 
-        def unless_late(y, place):
-            @pl.when(jnp.logical_and(place > 0, y * 4 + place != me))
-            def _():
-                send(y, place)
-
-        for y in order:
-            if 2 <= y < 6:
-                if c < FEW:
+        if y > 0:
+            to_others(y, send)
+        else:
+
+            @pl.when(band == 0)
+            def _():
+                for place in lows:
+                    unless_late(place)
+
+            @pl.when(band != 0)
+            def _():
+                to_others(y, send)
+
+    def send_rows(planes, rows):
+        for c in planes:
+            for y in rows:
+                if 2 <= y < 6:
                     for place in lows:
-                        send(y, place)
-            elif y > 0:
-                to_others(y, send)
-            else:
-
-                @pl.when(band == 0)
-                def _():
-                    for place in lows:
-                        unless_late(0, place)
-
-                @pl.when(band != 0)
-                def _():
-                    to_others(0, send)
+                        send_plane(c, y, place)
+                else:
+                    send_row(c, y)
 
     def send_columns(c):
         plane = plane_of(my_y, my_low, c)
@@ -647,7 +658,7 @@
 
         @pl.when(z_turn(z) < my_z_turn)
         def _():
-            hello(ready.at[0], {"band": my_x * 4 + z})
+            hello(ready.at[6 + my_z_turn], {"band": my_x * 4 + z})
             send_v_along_z(z, my_z_turn)
 
     for x in x_peers:
@@ -664,6 +675,20 @@
     def _():
         with jax.named_scope("planes"):
             to_planes()
+
+        with jax.named_scope("send_first"):
+
+            @pl.when(my_y == 1)
+            def _():
+                send_rows(FIRST, (0,))
+
+            @pl.when(my_y == 7)
+            def _():
+                send_rows(FIRST, (1, 0))
+
+            @pl.when(my_y == 6)
+            def _():
+                send_rows(FIRST, (1, 0, 7))
 
     def hand_on(z, later):
         @pl.when(active & (z_turn(z) > my_z_turn if later else z_turn(z) < my_z_turn) & jnp.logical_not((my_z >= 2) & (z < 2)))
@@ -681,12 +706,85 @@
         def _():
             send_v_directly(vbuf.at[4, my_rows, :], 8)
 
+    def own_along_x():
+        with jax.named_scope("wait_x"):
+            wait_for(ready.at[1], 3 - my_x_turn)
+        send_v_along_x(my_z)
+
+    def z_of(turn):
+        return jnp.abs(turn - z_shift) if turn < 2 else turn
+
+    def reach_z(turn):
+        @pl.when(turn > my_z_turn)
+        def _():
+            with jax.named_scope(f"wait_z{turn}"):
+                pl.semaphore_wait(ready.at[6 + turn], 1)
+            send_v_along_z(z_of(turn), my_z_turn)
+
+            @pl.when(jnp.logical_not(late))
+            def _():
+                hand_on(z_of(turn), True)
+
+    def forward_v(turn):
+        @pl.when(turn != my_z_turn if turn < 2 else jnp.logical_and(turn != my_z_turn, jnp.logical_not(early)))
+        def _():
+            with jax.named_scope(f"wait_vz{turn}"):
+                for_kind(lambda planes: v_along_z(planes, turn).wait_recv())
+            send_v_along_x(z_of(turn))
+
+    def know_late():
+        @pl.when(jnp.logical_and(band == 0, me > 0))
+        def _():
+            with jax.named_scope("wait_late"):
+                pl.semaphore_wait(ready.at[3], 1)
+
+            @pl.when(me == 8)
+            def _():
+                v_handed.start()
+
+            @pl.when(active)
+            def _():
+                for c in range(PLANES):
+                    send_plane(c, 0, 0)
+
+    @pl.when(active)
+    def _():
+        own_along_x()
+
+    @pl.when(jnp.logical_not(active))
+    def _():
+        own_along_x()
+        reach_z(1)
+        forward_v(0)
+        forward_v(1)
+        know_late()
+        reach_z(2)
+        reach_z(3)
+        forward_v(2)
+        forward_v(3)
+
+    with jax.named_scope("wait_rows"):
+        wait_for(ready.at[5], later_rows)
+
+    with jax.named_scope("send_rows"):
+
+        @pl.when(my_y == 0)
+        def _():
+            send_rows(FIRST, (6, 7, 1))
+
+        @pl.when(my_y == 1)
+        def _():
+            send_rows(FIRST, (6, 7))
+
+        @pl.when(my_y == 7)
+        def _():
+            send_rows(FIRST, (6,))
+
     with jax.named_scope("wait_group"):
         wait_for(
             ready.at[2],
-            jnp.where(late, 0, jnp.where(band == 0, FFT - 2, FFT - 1) - earlier - jnp.where(side_2, 8, 0)),
+            jnp.where(late, 0, jnp.where(band == 0, FFT - 2, FFT - 1) - earlier - jnp.where(side_2, 8, 0) - later_rows),
         )
-
 
     @pl.when(my_y == 1)
     def _():
@@ -695,81 +793,54 @@
 
     with jax.named_scope("send"):
 
+        rest = [c for c in range(PLANES) if c not in FIRST]
+
+        def own_row(planes):
+            for y in (0, 1, 6, 7):
+
+                @pl.when(my_y == y)
+                def _():
+                    send_rows(planes, (y,))
+
         @pl.when(my_y < 2)
         def _():
-            for c in range(PLANES):
-                send_planes(c, (4, 3, 5, 2, 6, 7, 1, 0))
+            send_rows((0,), (4, 3, 5, 2))
+            own_row(FIRST)
+            send_rows((1,), (4, 3, 5, 2))
+            send_rows(rest[:1], (6, 7, 1, 0))
+            send_rows((2,), (4, 3, 5, 2))
+            send_rows(rest[1:], (6, 7, 1, 0))
 
         @pl.when(side_6)
         def _():
-            for c in range(2):
-                send_planes(c, (4, 5, 1, 0, 6, 7))
+            send_rows((0,), (4, 5))
+            own_row(FIRST)
             pl.semaphore_wait(ready.at[4], 1)
-            for c in range(2):
-                send_planes(c, (3, 2))
-            for c in range(2, PLANES):
-                send_planes(c, (3, 4, 2, 5, 1, 0, 6, 7))
-
-    with jax.named_scope("wait_z"):
-        wait_for(ready.at[0], 3 - my_z_turn)
-
-    @pl.when(jnp.logical_not(late))
-    def _():
-        for z in z_peers:
-            hand_on(z, True)
-
-    for z in z_peers:
-
-        @pl.when(z_turn(z) > my_z_turn)
-        def _():
-            send_v_along_z(z, my_z_turn)
-
-    with jax.named_scope("wait_x"):
-        wait_for(ready.at[1], 3 - my_x_turn)
-    send_v_along_x(my_z)
+            send_rows((0,), (3, 2))
+            send_rows((1,), (3, 4, 2, 5))
+            send_rows(rest[:1], (1, 0, 7, 6))
+            send_rows((2,), (3, 4, 2, 5))
+            send_rows(rest[1:], (1, 0, 7, 6))
 
     @pl.when(active)
     def _():
+        reach_z(1)
+        forward_v(0)
+        forward_v(1)
+        know_late()
+        reach_z(2)
+        reach_z(3)
         with jax.named_scope("the_rest"):
             the_rest()
-
-    def forward_v(turn, z):
-        @pl.when(turn != my_z_turn if turn < 2 else jnp.logical_and(turn != my_z_turn, jnp.logical_not(early)))
-        def _():
-            with jax.named_scope(f"wait_vz{turn}"):
-                for_kind(lambda planes: v_along_z(planes, turn).wait_recv())
-            send_v_along_x(z)
-
-    def z_of(turn):
-        return jnp.abs(turn - z_shift) if turn < 2 else turn
-
-    for turn in range(2):
-        forward_v(turn, z_of(turn))
-
-    @pl.when(jnp.logical_and(band == 0, me > 0))
-    def _():
-        with jax.named_scope("wait_late"):
-            pl.semaphore_wait(ready.at[3], 1)
-
-        @pl.when(me == 8)
-        def _():
-            v_handed.start()
-
-        @pl.when(active)
-        def _():
-            for c in range(PLANES):
-                send_plane(c, 0, 0)
-
-    forward_v(2, z_of(2))
-
-    forward_v(3, z_of(3))
-
-    @pl.when(late)
-    def _():
-        v_handed.wait_recv()
-        for z in z_peers:
-            hand_on(z, False)
-            hand_on(z, True)
+        forward_v(2)
+        forward_v(3)
+
+        @pl.when(late)
+        def _():
+            v_handed.wait_recv()
+            for z in z_peers:
+                hand_on(z, False)
+                hand_on(z, True)
 
     for copy in table_copies[1:]:
         copy.wait()
@@ -937,7 +1008,7 @@
             dma((9,)),
             dma,
             dma,
-            pltpu.SemaphoreType.REGULAR((5,)),
+            pltpu.SemaphoreType.REGULAR((10,)),
         ],
         compiler_params=pltpu.CompilerParams(
             collective_id=0, has_side_effects=True, vmem_limit_bytes=24 * 1024 * 1024

time: 37.4 us -> 37.3 us (level)
  no operation moved by 1% of the time
where the time goes in v4:
time: 37.3 us; the launch traced here: 37.2 us
  Pallas kernels  35.9 us (96%)
  between operations  1.3 us (3%)
    pallas_call x1, Pallas kernels, local(): pl.pallas_call(kernel, out_shape=pltpu.VMEM((BANDS, 4, KEPT, N), f32), in...  34.8 us
    pallas_call x1, Pallas kernels, local(): pl.pallas_call(expand, out_shape=jax.ShapeDtypeStruct(wave.shape, f32), i...  1.09 us

profile of v4, /device:TPU:1, one launch (start us, length us, event | category | flops | bytes accessed | tf_op | source)
XLA Modules:
  0.0 37.2 jit_solution(16679122727188875177)
XLA Ops:
  1.3 34.8 %shard_map.127.packed = f32[2,4,64,128]{3,2,1,0:T(8,128)S(1)} custom-call(f32[2,2,4,128,128]{4,3,2,1,0:T(8,128)} %wave.1, f32[2,2,4,128,128]{4,3,2,1,0:T(8,128)} %previous.1, f32[32,128]{1,0:T(8,128)} %bitcast.1, s32[4,128]{1,0:T(4,128)} %extent_hbm.1, f32[3]{0:T(128)} %metric_hbm.1, f32[1]{0:T(128)S(6)} %copy.14.center, f32[1]{0:T(128)S(6)} %copy.15.halfwidth, ...), custom_call_target="tpu_custom_call" | custom-call | tf_op jit(solution)/shard_map/pallas_call | solution.py:975
  36.1 1.1 %shard_map.128 = f32[2,2,4,128,128]{4,3,2,1,0:T(8,128)} custom-call(f32[2,4,64,128]{3,2,1,0:T(8,128)S(1)} %shard_map.127.packed), custom_call_target="tpu_custom_call" | custom-call | tf_op jit(solution)/shard_map/pallas_call | solution.py:1025

commit v5 on v4

--- a/solution.py
+++ b/solution.py
@@ -18,6 +18,7 @@
 PLANES = 5
 FEW = 3
 FIRST = (0,)
+MESSAGES = 3 * (FFT - 1) + 2 * (ACTIVE - 1)
 MESH = pl.DeviceIdType.MESH
 
 
@@ -94,7 +95,7 @@
 
     cosine, sine = cos_sin(kept, grid)
     forward_z = stacked(cosine / N, sine / N)
-    return [inverse_z, inverse_y, inverse_x, forward_x, forward_y, forward_z]
+    return np.concatenate([inverse_z, inverse_y, inverse_x, forward_x, forward_y, forward_z], axis=0)
 
 
 def halves(value):
@@ -115,24 +116,14 @@
     metric_hbm,
     center,
     halfwidth,
-    iz_hbm,
-    iy_hbm,
-    ix_hbm,
-    fx_hbm,
-    fy_hbm,
-    fz_hbm,
+    tables_hbm,
     out,
     extent,
     metric,
     wbuf,
     pbuf,
     vbuf,
-    iz,
-    iy,
-    ix,
-    fx,
-    fy,
-    fz,
+    tables,
     vown,
     zboth,
     sbuf,
@@ -155,7 +146,6 @@
     grecv,
     vsend,
     vrecv,
-    esend,
     erecv,
     ready,
 ):
@@ -230,7 +220,7 @@
             if later or 2 <= y < 6:
                 pl.when(near)(lambda: row(semaphore))
             else:
-                pl.when(near & active)(lambda: row(ready.at[5]))
+                pl.when(near & active)(lambda: row(ready.at[4]))
                 pl.when(near & jnp.logical_not(active))(lambda: row(semaphore))
 
         for place in range(4):
@@ -292,7 +282,7 @@
             pltpu.make_async_copy(
                 wave.at[:, b, :, pl.ds(h * (N - HALF), HALF), :],
                 wbuf.at[:, b, :, pl.ds(h * HALF, HALF), :],
-                wsem.at[b, h],
+                wsem,
             )
             for h in range(2)
         ]
@@ -301,14 +291,18 @@
         pltpu.make_async_copy(
             previous.at[:, :, :, pl.ds(h * (N - HALF), HALF), :],
             pbuf.at[:, :, :, pl.ds(h * HALF, HALF), :],
-            psem.at[h],
+            psem,
         )
         for h in range(2)
     ]
     small_refs = ((extent_hbm, extent), (metric_hbm, metric))
     small_copies = [pltpu.make_async_copy(a, b, lsem.at[i + 1]) for i, (a, b) in enumerate(small_refs)]
-    table_refs = ((iz_hbm, iz), (iy_hbm, iy), (ix_hbm, ix), (fx_hbm, fx), (fy_hbm, fy), (fz_hbm, fz))
-    table_copies = [pltpu.make_async_copy(a, b, tsem.at[i]) for i, (a, b) in enumerate(table_refs)]
+    starts = (0, 256, 640, 896, 1152, 1408, 1664)
+    iz, iy, ix, fx, fy, fz = [tables.at[pl.ds(a, b - a), :] for a, b in zip(starts[:-1], starts[1:], strict=True)]
+    table_copies = [
+        pltpu.make_async_copy(tables_hbm.at[pl.ds(a, b - a), :], tables.at[pl.ds(a, b - a), :], tsem.at[i])
+        for i, (a, b) in enumerate(((0, 256), (256, 1664)))
+    ]
 
     for copy in small_copies:
         copy.start()
@@ -355,9 +349,7 @@
         return keep * real + pltpu.roll(keep * imag, KEPT, axis=1)
 
     def to_planes():
-        for b in range(BANDS):
-            for copy in wave_copies(b):
-                copy.wait()
+        pltpu.make_async_copy(wbuf, wbuf, wsem).wait()
         for j in range(4):
             keep = keep_of(j)
             for b in range(BANDS):
@@ -379,8 +371,7 @@
         return jnp.full((1, N), 2.0, jnp.float32) / jnp.full((1, N), halfwidth[0], jnp.float32)
 
     def the_rest():
-        for copy in previous_copies:
-            copy.wait()
+        pltpu.make_async_copy(pbuf, pbuf, psem).wait()
         step_z = (2.0 * math.pi / N) * signed_gz.astype(jnp.float32)
         step_y = (2.0 * math.pi / N) * signed_gy.astype(jnp.float32)
         plane_kinetic = metric[2] * (step_z * step_z) + metric[1] * (step_y * step_y)
@@ -399,7 +390,7 @@
         pltpu.make_async_remote_copy(
             src_ref=sbuf.at[pl.ds(pl.multiple_of(plane_of(y, place, c) * 8, 8), 8), :],
             dst_ref=rbuf.at[c, pl.ds(pl.multiple_of(slot * 8, 8), 8), :],
-            send_sem=fsend.at[c],
+            send_sem=fsend,
             recv_sem=frecv.at[c],
             device_id={"fft": y * 4 + place},
             device_id_type=MESH,
@@ -455,22 +446,22 @@
             pltpu.make_async_remote_copy(
                 src_ref=gbuf.at[c, pl.ds(pl.multiple_of((first + place) * 8, 8), 8), :],
                 dst_ref=hbuf.at[pl.ds(pl.multiple_of(plane * 8, 8), 8), :],
-                send_sem=gsend.at[c],
-                recv_sem=grecv.at[c],
+                send_sem=gsend,
+                recv_sem=grecv,
                 device_id={"fft": y * 4 + place},
                 device_id_type=MESH,
             ).start()
 
         @pl.when(active)
         def _():
-            for y in (7, 0, 6, 1):
+            for y in (0, 1, 7, 6):
                 to_others(y, send)
 
         if c < FEW:
 
             @pl.when(jnp.logical_not(active))
             def _():
-                for y in (7, 0, 6, 1):
+                for y in (0, 1, 7, 6):
                     for place in lows:
                         send(y, place)
 
@@ -483,7 +474,7 @@
         pltpu.make_async_remote_copy(
             src_ref=where,
             dst_ref=where,
-            send_sem=vsend.at[phase],
+            send_sem=vsend,
             recv_sem=vrecv.at[phase],
             device_id={"band": peer},
             device_id_type=MESH,
@@ -510,7 +501,7 @@
             for_kind(lambda planes: send_v(v_part(planes, my_rows), turn, my_x * 4 + z))
 
     def v_along_z(planes, turn):
-        return awaited(v_part(planes, pl.ds(0, 8)), vsend.at[turn], vrecv.at[turn])
+        return awaited(v_part(planes, pl.ds(0, 8)), vsend, vrecv.at[turn])
 
     def send_v_along_x(z):
         for x in x_peers:
@@ -522,15 +513,15 @@
                 send_v(part, phase, x * 4 + z)
 
     def v_wait(planes, phase, rows):
-        return awaited(v_part(planes, pl.ds(0, rows)), vsend.at[phase], vrecv.at[phase])
+        return awaited(v_part(planes, pl.ds(0, rows)), vsend, vrecv.at[phase])
 
     def v_last(phase, rows):
-        return awaited(vbuf.at[4, pl.ds(0, rows), :], vsend.at[phase], vrecv.at[phase])
+        return awaited(vbuf.at[4, pl.ds(0, rows), :], vsend, vrecv.at[phase])
 
     v_handed = pltpu.make_async_remote_copy(
         src_ref=vbuf.at[3, my_rows, :],
         dst_ref=vbuf.at[4, my_rows, :],
-        send_sem=esend,
+        send_sem=vsend,
         recv_sem=erecv,
         device_id={"fft": partner(my_y) * 4 + my_low},
         device_id_type=MESH,
@@ -541,13 +532,13 @@
 
             @pl.when(active)
             def _():
-                awaited(rbuf.at[c, pl.ds(0, 8 * (ACTIVE - 1)), :], fsend.at[c], frecv.at[c]).wait_recv()
+                awaited(rbuf.at[c, pl.ds(0, 8 * (ACTIVE - 1)), :], fsend, frecv.at[c]).wait_recv()
 
             if c < FEW:
 
                 @pl.when(jnp.logical_not(active))
                 def _():
-                    awaited(rbuf.at[c], fsend.at[c], frecv.at[c]).wait_recv()
+                    awaited(rbuf.at[c], fsend, frecv.at[c]).wait_recv()
 
         high, low = halves(rbuf[c])
         plane = dot(jnp.concatenate([high, low, high], axis=1), iy[...])
@@ -575,8 +566,7 @@
                 def arrived(planes):
                     @pl.when(early)
                     def _():
-                        v_wait(planes, 4, 48).wait_recv()
-                        v_wait(planes, 7, 64).wait_recv()
+                        v_wait(planes, 4, 112).wait_recv()
 
                     @pl.when(jnp.logical_not(early))
                     def _():
@@ -586,11 +576,9 @@
         if c == 4:
             with jax.named_scope("wait_v4"):
 
-
                 @pl.when(my_z < 2)
                 def _():
-                    v_last(6, 48).wait_recv()
-                    v_last(8, 64).wait_recv()
+                    v_last(6, 112).wait_recv()
 
                 @pl.when(my_z >= 2)
                 def _():
@@ -637,15 +625,15 @@
 
     @pl.when(tardy)
     def _():
-        send_v_directly(v_part(FEW, my_rows), 7)
+        send_v_directly(v_part(FEW, my_rows), 4)
 
     @pl.when(late)
     def _():
-        greet_all(ready.at[3])
+        greet_all(ready.at[2])
 
     @pl.when(jnp.logical_not(late))
     def _():
-        greet(ready.at[2], False)
+        greet(ready.at[1], False)
 
     waits_for_first = jnp.logical_and(band == 0, me == 8)
 
@@ -658,14 +646,14 @@
 
         @pl.when(z_turn(z) < my_z_turn)
         def _():
-            hello(ready.at[6 + my_z_turn], {"band": my_x * 4 + z})
+            hello(ready.at[4 + my_z_turn], {"band": my_x * 4 + z})
             send_v_along_z(z, my_z_turn)
 
     for x in x_peers:
 
         @pl.when(x_turn(x) < my_x_turn)
         def _():
-            hello(ready.at[1], {"band": x * 4 + my_z})
+            hello(ready.at[0], {"band": x * 4 + my_z})
 
     for copy in small_copies:
         copy.wait()
@@ -704,11 +692,11 @@
 
         @pl.when(my_z >= 2)
         def _():
-            send_v_directly(vbuf.at[4, my_rows, :], 8)
+            send_v_directly(vbuf.at[4, my_rows, :], 6)
 
     def own_along_x():
         with jax.named_scope("wait_x"):
-            wait_for(ready.at[1], 3 - my_x_turn)
+            wait_for(ready.at[0], 3 - my_x_turn)
         send_v_along_x(my_z)
 
     def z_of(turn):
@@ -718,7 +706,7 @@
         @pl.when(turn > my_z_turn)
         def _():
             with jax.named_scope(f"wait_z{turn}"):
-                pl.semaphore_wait(ready.at[6 + turn], 1)
+                pl.semaphore_wait(ready.at[4 + turn], 1)
             send_v_along_z(z_of(turn), my_z_turn)
 
             @pl.when(jnp.logical_not(late))
@@ -736,7 +724,7 @@
         @pl.when(jnp.logical_and(band == 0, me > 0))
         def _():
             with jax.named_scope("wait_late"):
-                pl.semaphore_wait(ready.at[3], 1)
+                pl.semaphore_wait(ready.at[2], 1)
 
             @pl.when(me == 8)
             def _():
@@ -764,7 +752,7 @@
         forward_v(3)
 
     with jax.named_scope("wait_rows"):
-        wait_for(ready.at[5], later_rows)
+        wait_for(ready.at[4], later_rows)
 
     with jax.named_scope("send_rows"):
 
@@ -782,14 +770,14 @@
 
     with jax.named_scope("wait_group"):
         wait_for(
-            ready.at[2],
+            ready.at[1],
             jnp.where(late, 0, jnp.where(band == 0, FFT - 2, FFT - 1) - earlier - jnp.where(side_2, 8, 0) - later_rows),
         )
 
     @pl.when(my_y == 1)
     def _():
         for y in (7, 6):
-            hello(ready.at[4], {"fft": y * 4 + my_low})
+            hello(ready.at[3], {"fft": y * 4 + my_low})
 
     with jax.named_scope("send"):
 
@@ -815,7 +803,7 @@
         def _():
             send_rows((0,), (4, 5))
             own_row(FIRST)
-            pl.semaphore_wait(ready.at[4], 1)
+            pl.semaphore_wait(ready.at[3], 1)
             send_rows((0,), (3, 2))
             send_rows((1,), (3, 4, 2, 5))
             send_rows(rest[:1], (1, 0, 7, 6))
@@ -871,9 +859,8 @@
             field(c)
             back(c)
         factor = scale()
-        for c in range(PLANES):
-            with jax.named_scope(f"wait_columns{c}"):
-                awaited(hbuf.at[pl.ds(0, 8 * peers_with(c)), :], gsend.at[c], grecv.at[c]).wait_recv()
+        with jax.named_scope("wait_columns"):
+            awaited(hbuf.at[pl.ds(0, 8 * MESSAGES), :], gsend, grecv).wait_recv()
         for j in range(4):
             h0, l0 = halves(hbuf[pl.ds(2 * j, N, stride=8), :])
             h1, l1 = halves(hbuf[pl.ds(2 * j + 1, N, stride=8), :])
@@ -892,49 +879,21 @@
 
     with jax.named_scope("wait_sends"):
 
+        def v_sent(rows):
+            awaited(hbuf.at[pl.ds(0, rows), :], vsend, erecv).wait_send()
+
         @pl.when(active)
         def _():
-
-            @pl.when(my_z < 2)
-            def _():
-                v_last(5, 24).wait_send()
-                v_last(6, 48).wait_send()
-
-            @pl.when(my_z >= 2)
-            def _():
-                v_last(5, 8).wait_send()
-                v_last(6, 96).wait_send()
-                v_last(8, 64).wait_send()
-
-            for c in range(PLANES):
-                awaited(sbuf.at[pl.ds(0, 8 * peers_with(c)), :], fsend.at[c], frecv.at[c]).wait_send()
-                awaited(gbuf.at[c, pl.ds(0, 8 * (ACTIVE - 1)), :], gsend.at[c], grecv.at[c]).wait_send()
+            awaited(sbuf.at[pl.ds(0, 8 * MESSAGES), :], fsend, erecv).wait_send()
+            awaited(gbuf.at[:, pl.ds(0, 8 * (ACTIVE - 1)), :], gsend, erecv).wait_send()
+            pl.when(my_z < 2)(lambda: v_sent(552))
+            pl.when(my_z >= 2)(lambda: v_sent(648))
 
         @pl.when(jnp.logical_not(active))
         def _():
-            v_handed.wait_send()
-            for c in range(FEW):
-                awaited(gbuf.at[c], gsend.at[c], grecv.at[c]).wait_send()
-
-        def v_sent(planes):
-            @pl.when(early)
-            def _():
-                v_wait(planes, 4, 48).wait_send()
-
-            @pl.when(jnp.logical_not(early))
-            def _():
-                v_wait(planes, 4, 96).wait_send()
-
-            @pl.when(tardy)
-            def _():
-                awaited(v_part(planes, pl.ds(0, 8)), vsend.at[my_z_turn], vrecv.at[4]).wait_send()
-                v_wait(planes, 7, 64).wait_send()
-
-            @pl.when(jnp.logical_not(tardy))
-            def _():
-                awaited(v_part(planes, pl.ds(0, 24)), vsend.at[my_z_turn], vrecv.at[4]).wait_send()
-
-        for_kind(v_sent)
+            awaited(gbuf.at[pl.ds(0, FEW), :, :], gsend, erecv).wait_send()
+            pl.when(early)(lambda: v_sent(224))
+            pl.when(tardy)(lambda: v_sent(512))
 
 
 def expand(packed, out, obuf, sem):
@@ -975,7 +934,7 @@
     packed = pl.pallas_call(
         kernel,
         out_shape=pltpu.VMEM((BANDS, 4, KEPT, N), f32),
-        in_specs=[any_spec] * 5 + [smem_spec] * 2 + [any_spec] * 6,
+        in_specs=[any_spec] * 5 + [smem_spec] * 2 + [any_spec],
         out_specs=vmem_spec,
         scratch_shapes=[
             pltpu.VMEM((4, N), jnp.int32),
@@ -983,7 +942,7 @@
             pltpu.VMEM((2, BANDS, 4, KEPT, N), f32),
             pltpu.VMEM((2, BANDS, 4, KEPT, N), f32),
             pltpu.VMEM((PLANES, N, N), f32),
-            *[pltpu.VMEM(table.shape, bf16) for table in tables],
+            pltpu.VMEM(tables.shape, bf16),
             pltpu.VMEM((32, N), f32),
             pltpu.VMEM((4, 2 * N, 2 * N), bf16),
             pltpu.VMEM((8 * N, N), f32),
@@ -996,19 +955,18 @@
             pltpu.VMEM((PLANES, N, N), f32),
             pltpu.VMEM((8 * N, N), f32),
             pltpu.VMEM((BANDS, 4, KEPT, N), f32),
-            dma((BANDS, 2)),
-            dma((2,)),
-            dma((6,)),
-            dma((3,)),
-            dma((PLANES,)),
-            dma((PLANES,)),
-            dma((PLANES,)),
-            dma((PLANES,)),
-            dma((9,)),
-            dma((9,)),
             dma,
             dma,
-            pltpu.SemaphoreType.REGULAR((10,)),
+            dma((2,)),
+            dma((3,)),
+            dma,
+            dma((PLANES,)),
+            dma,
+            dma,
+            dma,
+            dma((7,)),
+            dma,
+            pltpu.SemaphoreType.REGULAR((8,)),
         ],
         compiler_params=pltpu.CompilerParams(
             collective_id=0, has_side_effects=True, vmem_limit_bytes=24 * 1024 * 1024
@@ -1020,7 +978,7 @@
         ],
         center,
         halfwidth,
-        *[pltpu.with_memory_space_constraint(table, pltpu.HBM) for table in tables],
+        pltpu.with_memory_space_constraint(tables, pltpu.HBM),
     )
     return pl.pallas_call(
         expand,
@@ -1033,7 +991,7 @@
 
 
 def solution(mesh):
-    tables = [jnp.asarray(table) for table in make_tables()]
+    tables = jnp.asarray(make_tables())
     in_specs = (
         P(None, "band", "fft", None, None),
         P(None, "band", "fft", None, None),

time: 37.3 us -> 36.8 us (0.987)
  Pallas kernels: 35.9 us -> 35.4 us
    pallas_call x1, Pallas kernels: 34.8 us -> 34.3 us  [local(): pl.pallas_call(kernel, out_shape=pltpu.VMEM((BANDS, 4, KEPT, N), f32), in...]
where the time goes in v5:
time: 36.8 us; the launch traced here: 36.7 us
  Pallas kernels  35.4 us (96%)
  between operations  1.3 us (4%)
    pallas_call x1, Pallas kernels, local(): pl.pallas_call(kernel, out_shape=pltpu.VMEM((BANDS, 4, KEPT, N), f32), in...  34.3 us
    pallas_call x1, Pallas kernels, local(): pl.pallas_call(expand, out_shape=jax.ShapeDtypeStruct(wave.shape, f32), i...  1.09 us

profile of v5, /device:TPU:1, one launch (start us, length us, event | category | flops | bytes accessed | tf_op | source)
XLA Modules:
  0.0 36.7 jit_solution(15687761077782537392)
XLA Ops:
  1.3 34.3 %shard_map.82.packed = f32[2,4,64,128]{3,2,1,0:T(8,128)S(1)} custom-call(f32[2,2,4,128,128]{4,3,2,1,0:T(8,128)} %wave.1, f32[2,2,4,128,128]{4,3,2,1,0:T(8,128)} %previous.1, f32[32,128]{1,0:T(8,128)} %bitcast.1, s32[4,128]{1,0:T(4,128)} %extent_hbm.1, f32[3]{0:T(128)} %metric_hbm.1, f32[1]{0:T(128)S(6)} %copy.9.center, f32[1]{0:T(128)S(6)} %copy.10.halfwidth, ...), custom_call_target="tpu_custom_call" | custom-call | tf_op jit(solution)/shard_map/pallas_call | solution.py:934
  35.6 1.1 %shard_map.83 = f32[2,2,4,128,128]{4,3,2,1,0:T(8,128)} custom-call(f32[2,4,64,128]{3,2,1,0:T(8,128)S(1)} %shard_map.82.packed), custom_call_target="tpu_custom_call" | custom-call | tf_op jit(solution)/shard_map/pallas_call | solution.py:983
